TPU v7x, 32 devices: a whole 2x2x4 slice. The times are simulated.
32 devices in a mesh: tok: 4 (over x, core), col: 8 (over z, y).
Axes of the slice: x: 2, y: 2, z: 4, core: 2. Of those that a mesh axis runs over, the one named last changes fastest.
Arguments:
- hidden_in: bfloat16 [1024, 36864], P('tok', 'col'), may hold values from -6 to 6
- down_weight: bfloat16 [4608, 36864], P('col', 'tok'), may hold values from -0.046875 to 0.046875
- keep_mask: int32 [4608, 36864], P('col', 'tok'), may hold values 0 or 1
Outputs:
- layer_out: bfloat16 [1024, 4608], P(('tok', 'col'))
- hessian: float32 [4608, 4608], P('col', 'tok')
All inputs are finite; a program needn't handle non-finite values. No bound on the sum of `keep_mask` on one device may be relied on, other than what follows from the above.
Results may differ from a plain program's by a relative error of at most 0.012.
Values may be sent and summed in bfloat16 or wider, within the bound.
No kernel may reach another device: no remote copies, remote signals or barrier semaphores. Data moves between devices by JAX's collectives and lax.ppermute only.
A program may use at most 192 MiB of HBM per device.

v0:
```python
import functools

import jax
import jax.numpy as jnp
from jax import lax
from jax.experimental import pallas as pl
from jax.experimental.pallas import tpu as pltpu
from jax.sharding import Mesh, PartitionSpec as P


SHARES = (4, 4, 4, 2, 2)
GROUPS = ((0, 1, 2), (3, 4))


def swap(value, axis, offset):
    return lax.ppermute(value, axis, [(i, i ^ offset) for i in range(lax.axis_size(axis))])


def spread_first(value, axis):
    size = lax.axis_size(axis)
    if size != 4:
        return [value] + [swap(value, axis, k) for k in range(1, size)]
    near, far = swap(value, axis, 1), swap(value, axis, 2)
    return [value, near, far, lax.ppermute(value, axis, [(1, 2), (2, 1)])]


def spread_last(blocks, axis):
    if lax.axis_size(axis) != 4:
        return blocks
    return list(blocks) + [lax.ppermute(blocks[2], axis, [(1, 0), (2, 3)])]


def spread(value, axis):
    return spread_last(spread_first(value, axis), axis)


def order_kernel(size, by_ref, *refs):
    outs = refs[len(refs) - size :]
    blocks = refs[: len(refs) - size]

    def write(by, last):
        for k in range(size):
            at = k ^ by
            outs[k][...] = blocks[last if at == size - 1 else at][...]

    for by in range(size):
        if len(blocks) == size:
            pl.when(by_ref[0] == by)(functools.partial(write, by, size - 1))
        else:
            for end in range(2):
                pl.when((by_ref[0] == by) & (by_ref[1] == end))(functools.partial(write, by, size - 1 + end))


def xor_order(blocks, by, axis):
    size, index = lax.axis_size(axis), lax.axis_index(axis)
    at_end = (index == 0) | (index == size - 1)
    rows, cols = blocks[0].shape
    tile = 16 if rows % 16 == 0 and cols >= 2048 else rows
    spec = pl.BlockSpec((tile, cols), lambda i, by: (i, 0))
    return pl.pallas_call(
        functools.partial(order_kernel, size),
        grid_spec=pltpu.PrefetchScalarGridSpec(
            num_scalar_prefetch=1, grid=(rows // tile,), in_specs=[spec] * len(blocks), out_specs=[spec] * size
        ),
        out_shape=[jax.ShapeDtypeStruct((rows, cols), blocks[0].dtype)] * size,
        cost_estimate=pl.CostEstimate(flops=rows * cols * size, bytes_accessed=4 * rows * cols * size, transcendentals=0),
    )(jnp.stack([by, at_end.astype(jnp.int32)]), *blocks)


def turn(blocks, axis):
    return list(blocks[:1]) + [swap(blocks[k], axis, k) for k in range(1, len(blocks))]


def contract_last(left, right):
    return lax.dot_general(left, right, (((1,), (1,)), ((), ())), preferred_element_type=jnp.float32)


def contract_rows(left, right):
    return lax.dot_general(left, right, (((0,), (0,)), ((), ())), preferred_element_type=jnp.float32)


def body(hidden_in, down_weight, keep_mask):
    tok, row, sub = lax.axis_index("tok"), lax.axis_index("row"), lax.axis_index("sub")
    toks, subs = lax.axis_size("tok"), lax.axis_size("sub")
    rows, depth = hidden_in.shape
    cols = down_weight.shape[0]
    small = jnp.bfloat16
    steps = [rows * share // sum(SHARES) for share in SHARES]
    starts = [sum(steps[:j]) for j in range(len(steps))]

    def pruned(weight, mask, block):
        w = lax.dynamic_slice(weight, (0, block * depth), (cols, depth))
        return w * lax.dynamic_slice(mask, (0, block * depth), (cols, depth)).astype(w.dtype)

    pieces = lax.optimization_barrier([hidden_in[at : at + n] for at, n in zip(starts, steps)])
    seen = [spread_first(piece, "row") for piece in pieces]

    sent = [swap(pruned(down_weight, keep_mask, sub ^ k), "sub", k) for k in range(1, subs)]
    weight, mask, _ = lax.optimization_barrier((down_weight, keep_mask, seen[0][1]))
    weights = [pruned(weight, mask, sub)] + sent

    shares = [[] for _ in range(subs)]
    for j in range(len(steps)):
        blocks = spread_last(seen[j], "row")
        chunk = jnp.concatenate(turn(xor_order(blocks, tok ^ row, "row"), "tok"), axis=0)
        for k in range(subs):
            shares[k].append(contract_last(chunk, weights[k]))

    left, right, layer_rows = [], [], []
    for group in GROUPS:

        def take(k):
            parts = [shares[k][j].reshape(toks, steps[j], cols) for j in group]
            return jnp.concatenate(parts, axis=1) if len(parts) > 1 else parts[0]

        total = take(0)
        for k in range(1, subs):
            total = total + swap(take(k).astype(small), "sub", k).astype(jnp.float32)
        rest = total[1:].astype(small)
        layer = total[0]
        for k in range(1, toks):
            layer = layer + swap(rest[k - 1], "tok", k).astype(jnp.float32)
        layer = layer.astype(small)
        blocks = spread(layer, "row")
        left.append(jnp.concatenate(turn([layer] * toks, "tok"), axis=0))
        layer_rows.append(blocks)
        mine = jnp.concatenate(turn(xor_order(blocks, tok ^ row, "row"), "tok"), axis=0)
        both = [mine] + [swap(mine, "sub", k) for k in range(1, subs)]
        right.append(jnp.concatenate(xor_order(both, sub, "sub"), axis=1))

    scaling = 2.0 / (rows * toks)
    hessian = contract_rows(jnp.concatenate(left, axis=0), jnp.concatenate(right, axis=0)) * scaling

    share = rows // (toks * subs)
    whole = [jnp.concatenate(blocks, axis=0) for blocks in zip(*layer_rows)]
    whole = jnp.stack(xor_order(whole, row, "row"), axis=0).reshape(toks, toks, subs, share, cols)

    def for_sub(other):
        return lax.dynamic_slice(whole, (0, row, other, 0, 0), (toks, 1, 1, share, cols)).reshape(toks * share, cols)

    pieces = [for_sub(sub)] + [swap(for_sub(sub ^ k), "sub", k) for k in range(1, subs)]
    pieces = [piece.reshape(toks, share, cols) for piece in xor_order(pieces, sub, "sub")]
    layer_out = jnp.stack(pieces, axis=1).transpose(2, 0, 1, 3).reshape(share, toks * subs * cols)
    return layer_out, hessian


def solution(mesh):
    toks, both = mesh.shape["tok"], mesh.shape["col"]
    subs = both // toks
    grid = Mesh(mesh.devices.reshape(toks, toks, subs), ("tok", "row", "sub"))
    col = ("row", "sub")
    in_specs = (P("tok", col), P(col, "tok"), P(col, "tok"))
    out_specs = (P(("tok",) + col, None), P(col, "tok"))
    return jax.shard_map(body, mesh=grid, in_specs=in_specs, out_specs=out_specs, check_vma=False)
```

profile of v0, /device:TPU:0, one launch (start us, length us, event | category | flops | bytes accessed | tf_op | source)
XLA Modules:
  0.0 481.9 jit_solution(665840677865042390)
XLA Ops:
  13.2 9.5 %fusion.1 = bf16[576,4608]{1,0:T(8,128)(2,1)} fusion(s32[576,9216]{1,0:T(8,128)} %param.5, s32[]{:T(128)S(6)} %select_n.19, bf16[576,9216]{1,0:T(8,128)(2,1)} %param.4), kind=kLoop, calls=%fused_computation.3 | loop fusion | flops 13271040 | bytes 21233668 | tf_op jit(solution)/shard_map/mul | solution.py:93
  27.4 25.2 %collective-permute-done.refs_1_ = bf16[64,4608]{1,0:T(8,128)(2,1)S(1)} collective-permute-done((bf16[64,4608]{1,0:T(8,128)(2,1)S(1)}, bf16[64,4608]{1,0:T(8,128)(2,1)S(1)}, u32[]{:S(2)}, u32[]{:S(2)}) %collective-permute-start) | collective-permute-done | bytes 589856 | tf_op jit(solution)/shard_map/ppermute | solution.py:16
  53.9 9.6 %fusion = bf16[576,4608]{1,0:T(8,128)(2,1)} fusion(s32[576,9216]{1,0:T(8,128)} %param.5, s32[]{:T(128)S(6)} %select_n.18, bf16[576,9216]{1,0:T(8,128)(2,1)} %param.4), kind=kLoop, calls=%fused_computation.2 | loop fusion | flops 13271040 | bytes 21233668 | tf_op jit(solution)/shard_map/mul | solution.py:93
  74.6 11.9 %collective-permute-done.26.refs_1_ = bf16[32,4608]{1,0:T(8,128)(2,1)S(1)} collective-permute-done((bf16[32,4608]{1,0:T(8,128)(2,1)S(1)}, bf16[32,4608]{1,0:T(8,128)(2,1)S(1)}, u32[]{:S(2)}, u32[]{:S(2)}) %collective-permute-start.26) | collective-permute-done | bytes 294944 | tf_op jit(solution)/shard_map/ppermute | solution.py:16
  88.0 14.6 %collective-permute-start.1 = (bf16[64,4608]{1,0:T(8,128)(2,1)S(1)}, bf16[64,4608]{1,0:T(8,128)(2,1)}, u32[]{:S(2)}, u32[]{:S(2)}) collective-permute-start(bf16[64,4608]{1,0:T(8,128)(2,1)S(1)} %get-tuple-element.47.refs_0_), channel_id=1, source_target_pairs={{0,4},{2,6},{4,0},{6,2},{1,5},{3,7},{5,1},{7,3},{8,12},{10,14},{12... | collective-permute-start | bytes 1769480 | tf_op jit(solution)/shard_map/ppermute | solution.py:16
  109.0 7.4 %collective-permute-done.38 = bf16[32,4608]{1,0:T(8,128)(2,1)S(1)} collective-permute-done((bf16[32,4608]{1,0:T(8,128)(2,1)}, bf16[32,4608]{1,0:T(8,128)(2,1)S(1)}, u32[]{:S(2)}, u32[]{:S(2)}) %collective-permute-start.38) | collective-permute-done | bytes 294944 | tf_op jit(solution)/shard_map/ppermute | solution.py:16
  116.4 9.5 %collective-permute-done.39 = bf16[32,4608]{1,0:T(8,128)(2,1)S(1)} collective-permute-done((bf16[32,4608]{1,0:T(8,128)(2,1)}, bf16[32,4608]{1,0:T(8,128)(2,1)S(1)}, u32[]{:S(2)}, u32[]{:S(2)}) %collective-permute-start.39) | collective-permute-done | bytes 294944 | tf_op jit(solution)/shard_map/ppermute | solution.py:16
  128.3 8.5 %collective-permute-done.31 = bf16[32,4608]{1,0:T(8,128)(2,1)S(1)} collective-permute-done((bf16[32,4608]{1,0:T(8,128)(2,1)S(1)}, bf16[32,4608]{1,0:T(8,128)(2,1)S(1)}, u32[]{:S(2)}, u32[]{:S(2)}) %collective-permute-start.31) | collective-permute-done | bytes 294944 | tf_op jit(solution)/shard_map/ppermute | solution.py:16
  137.0 8.8 %collective-permute-done.32 = bf16[32,4608]{1,0:T(8,128)(2,1)S(1)} collective-permute-done((bf16[32,4608]{1,0:T(8,128)(2,1)S(1)}, bf16[32,4608]{1,0:T(8,128)(2,1)S(1)}, u32[]{:S(2)}, u32[]{:S(2)}) %collective-permute-start.32) | collective-permute-done | bytes 294944 | tf_op jit(solution)/shard_map/ppermute | solution.py:16
  157.4 7.2 %collective-permute-done.8.refs_2_ = bf16[64,4608]{1,0:T(8,128)(2,1)} collective-permute-done((bf16[64,4608]{1,0:T(8,128)(2,1)}, bf16[64,4608]{1,0:T(8,128)(2,1)}, u32[]{:S(2)}, u32[]{:S(2)}) %collective-permute-start.8) | collective-permute-done | bytes 589856 | tf_op jit(solution)/shard_map/ppermute | solution.py:16
  170.0 6.7 %collective-permute-done.17.refs_4_ = bf16[64,4608]{1,0:T(8,128)(2,1)} collective-permute-done((bf16[64,4608]{1,0:T(8,128)(2,1)}, bf16[64,4608]{1,0:T(8,128)(2,1)}, u32[]{:S(2)}, u32[]{:S(2)}) %collective-permute-start.17) | collective-permute-done | bytes 589856 | tf_op jit(solution)/shard_map/ppermute | solution.py:30
  190.8 11.2 %collective-permute-done.10.refs_4_ = bf16[64,4608]{1,0:T(8,128)(2,1)} collective-permute-done((bf16[64,4608]{1,0:T(8,128)(2,1)}, bf16[64,4608]{1,0:T(8,128)(2,1)}, u32[]{:S(2)}, u32[]{:S(2)}) %collective-permute-start.10) | collective-permute-done | bytes 589856 | tf_op jit(solution)/shard_map/ppermute | solution.py:30
  235.1 8.2 %collective-permute-done.12 = bf16[64,4608]{1,0:T(8,128)(2,1)S(1)} collective-permute-done((bf16[64,4608]{1,0:T(8,128)(2,1)}, bf16[64,4608]{1,0:T(8,128)(2,1)S(1)}, u32[]{:S(2)}, u32[]{:S(2)}) %collective-permute-start.12) | collective-permute-done | bytes 589856 | tf_op jit(solution)/shard_map/ppermute | solution.py:16
  243.4 11.2 %collective-permute-done.13 = bf16[64,4608]{1,0:T(8,128)(2,1)S(1)} collective-permute-done((bf16[64,4608]{1,0:T(8,128)(2,1)S(1)}, bf16[64,4608]{1,0:T(8,128)(2,1)S(1)}, u32[]{:S(2)}, u32[]{:S(2)}) %collective-permute-start.13) | collective-permute-done | bytes 589856 | tf_op jit(solution)/shard_map/ppermute | solution.py:16
  254.7 13.9 %collective-permute-done.5 = bf16[64,4608]{1,0:T(8,128)(2,1)S(1)} collective-permute-done((bf16[64,4608]{1,0:T(8,128)(2,1)S(1)}, bf16[64,4608]{1,0:T(8,128)(2,1)S(1)}, u32[]{:S(2)}, u32[]{:S(2)}) %collective-permute-start.5) | collective-permute-done | bytes 589856 | tf_op jit(solution)/shard_map/ppermute | solution.py:16
  268.6 9.1 %collective-permute-done.6 = bf16[64,4608]{1,0:T(8,128)(2,1)S(1)} collective-permute-done((bf16[64,4608]{1,0:T(8,128)(2,1)S(1)}, bf16[64,4608]{1,0:T(8,128)(2,1)S(1)}, u32[]{:S(2)}, u32[]{:S(2)}) %collective-permute-start.6) | collective-permute-done | bytes 589856 | tf_op jit(solution)/shard_map/ppermute | solution.py:16
  286.6 17.4 %collective-permute-done.21 = bf16[576,4608]{1,0:T(8,128)(2,1)} collective-permute-done((bf16[576,4608]{1,0:T(8,128)(2,1)}, bf16[576,4608]{1,0:T(8,128)(2,1)}, u32[]{:S(2)}, u32[]{:S(2)}) %collective-permute-start.21) | collective-permute-done | bytes 5308448 | tf_op jit(solution)/shard_map/ppermute | solution.py:16
  333.1 12.3 %collective-permute-done.22 = bf16[4,192,576]{2,1,0:T(8,128)(2,1)S(1)} collective-permute-done((bf16[4,192,576]{2,1,0:T(8,128)(2,1)}, bf16[4,192,576]{2,1,0:T(8,128)(2,1)S(1)}, u32[]{:S(2)}, u32[]{:S(2)}) %collective-permute-start.22) | collective-permute-done | bytes 884768 | tf_op jit(solution)/shard_map/ppermute | solution.py:16
  354.9 5.8 %collective-permute-done.24 = bf16[192,576]{1,0:T(8,128)(2,1)S(1)} collective-permute-done((bf16[192,576]{1,0:T(8,128)(2,1)S(1)}, bf16[192,576]{1,0:T(8,128)(2,1)S(1)}, u32[]{:S(2)}, u32[]{:S(2)}) %collective-permute-start.24) | collective-permute-done | bytes 221216 | tf_op jit(solution)/shard_map/ppermute | solution.py:16
  369.9 7.7 %collective-permute-done.55 = bf16[192,576]{1,0:T(8,128)(2,1)S(1)} collective-permute-done((bf16[192,576]{1,0:T(8,128)(2,1)S(1)}, bf16[192,576]{1,0:T(8,128)(2,1)S(1)}, u32[]{:S(2)}, u32[]{:S(2)}) %collective-permute-start.55) | collective-permute-done | bytes 221216 | tf_op jit(solution)/shard_map/ppermute | solution.py:16
  386.7 6.0 %collective-permute-done.46.refs_2_ = bf16[192,576]{1,0:T(8,128)(2,1)S(1)} collective-permute-done((bf16[192,576]{1,0:T(8,128)(2,1)S(1)}, bf16[192,576]{1,0:T(8,128)(2,1)S(1)}, u32[]{:S(2)}, u32[]{:S(2)}) %collective-permute-start.46) | collective-permute-done | bytes 221216 | tf_op jit(solution)/shard_map/ppermute | solution.py:16
  393.0 6.7 %collective-permute-done.47.refs_2_ = bf16[64,576]{1,0:T(8,128)(2,1)S(1)} collective-permute-done((bf16[64,576]{1,0:T(8,128)(2,1)S(1)}, bf16[64,576]{1,0:T(8,128)(2,1)S(1)}, u32[]{:S(2)}, u32[]{:S(2)}) %collective-permute-start.47) | collective-permute-done | bytes 73760 | tf_op jit(solution)/shard_map/ppermute | solution.py:16
  405.0 7.4 %collective-permute-done.51.refs_4_ = bf16[64,576]{1,0:T(8,128)(2,1)S(1)} collective-permute-done((bf16[64,576]{1,0:T(8,128)(2,1)S(1)}, bf16[64,576]{1,0:T(8,128)(2,1)S(1)}, u32[]{:S(2)}, u32[]{:S(2)}) %collective-permute-start.51) | collective-permute-done | bytes 73760 | tf_op jit(solution)/shard_map/ppermute | solution.py:30
  448.7 13.9 %collective-permute-done.52.refs_1_ = bf16[128,576]{1,0:T(8,128)(2,1)S(1)} collective-permute-done((bf16[128,576]{1,0:T(8,128)(2,1)S(1)}, bf16[128,576]{1,0:T(8,128)(2,1)S(1)}, u32[]{:S(2)}, u32[]{:S(2)}) %collective-permute-start.52) | collective-permute-done | bytes 147488 | tf_op jit(solution)/shard_map/ppermute | solution.py:16
  (297 shorter events, 230.7 us)
Async XLA Ops:
  4.5 58.9 %collective-permute-start.33 = (bf16[32,4608]{1,0:T(8,128)(2,1)S(1)}, bf16[32,4608]{1,0:T(8,128)(2,1)S(1)}, u32[]{:S(2)}, u32[]{:S(2)}) collective-permute-start(bf16[32,4608]{1,0:T(8,128)(2,1)S(1)} %get-tuple-element.69.refs_0_), channel_id=1, source_target_pairs={{0,2},{2,0},{4,6},{6,4},{1,3},{3,1},{5,7},{7,5},{8,10},{10,8},{12,... | collective-permute-start | bytes 884744 | tf_op jit(solution)/shard_map/ppermute | solution.py:16
  10.2 58.2 %collective-permute-start.35 = (bf16[32,4608]{1,0:T(8,128)(2,1)S(1)}, bf16[32,4608]{1,0:T(8,128)(2,1)S(1)}, u32[]{:S(2)}, u32[]{:S(2)}) collective-permute-start(bf16[32,4608]{1,0:T(8,128)(2,1)S(1)} %get-tuple-element.69.refs_0_), channel_id=1, source_target_pairs={{2,4},{4,2},{3,5},{5,3},{10,12},{12,10},{11,13},{13,11},{18,20},{2... | collective-permute-start | bytes 884744 | tf_op jit(solution)/shard_map/ppermute | solution.py:24
  10.9 141.5 %collective-permute-start.14 = (bf16[64,4608]{1,0:T(8,128)(2,1)}, bf16[64,4608]{1,0:T(8,128)(2,1)}, u32[]{:S(2)}, u32[]{:S(2)}) collective-permute-start(bf16[64,4608]{1,0:T(8,128)(2,1)} %get-tuple-element.59.refs_0_), channel_id=1, source_target_pairs={{0,2},{2,0},{4,6},{6,4},{1,3},{3,1},{5,7},{7,5},{8,10},{10,8},{12,... | collective-permute-start | bytes 1769480 | tf_op jit(solution)/shard_map/ppermute | solution.py:16
  13.1 39.5 %collective-permute-start = (bf16[64,4608]{1,0:T(8,128)(2,1)S(1)}, bf16[64,4608]{1,0:T(8,128)(2,1)S(1)}, u32[]{:S(2)}, u32[]{:S(2)}) collective-permute-start(bf16[64,4608]{1,0:T(8,128)(2,1)S(1)} %get-tuple-element.47.refs_0_), channel_id=1, source_target_pairs={{0,2},{2,0},{4,6},{6,4},{1,3},{3,1},{5,7},{7,5},{8,10},{10,8},{12,... | collective-permute-start | bytes 1769480 | tf_op jit(solution)/shard_map/ppermute | solution.py:16
  24.7 43.7 %collective-permute-start.27 = (bf16[32,4608]{1,0:T(8,128)(2,1)S(1)}, bf16[32,4608]{1,0:T(8,128)(2,1)}, u32[]{:S(2)}, u32[]{:S(2)}) collective-permute-start(bf16[32,4608]{1,0:T(8,128)(2,1)S(1)} %get-tuple-element.64.refs_0_), channel_id=1, source_target_pairs={{0,4},{2,6},{4,0},{6,2},{1,5},{3,7},{5,1},{7,3},{8,12},{10,14},{12... | collective-permute-start | bytes 884744 | tf_op jit(solution)/shard_map/ppermute | solution.py:16
  63.4 73.4 %collective-permute-start.15 = (bf16[64,4608]{1,0:T(8,128)(2,1)}, bf16[64,4608]{1,0:T(8,128)(2,1)}, u32[]{:S(2)}, u32[]{:S(2)}) collective-permute-start(bf16[64,4608]{1,0:T(8,128)(2,1)} %get-tuple-element.59.refs_0_), channel_id=1, source_target_pairs={{0,4},{2,6},{4,0},{6,2},{1,5},{3,7},{5,1},{7,3},{8,12},{10,14},{12... | collective-permute-start | bytes 1769480 | tf_op jit(solution)/shard_map/ppermute | solution.py:16
  69.2 33.4 %collective-permute-start.29 = (bf16[32,4608]{1,0:T(8,128)(2,1)}, bf16[32,4608]{1,0:T(8,128)(2,1)S(1)}, u32[]{:S(2)}, u32[]{:S(2)}) collective-permute-start(bf16[32,4608]{1,0:T(8,128)(2,1)} %collective-permute-done.27.refs_2_), channel_id=1, source_target_pairs={{2,0},{4,6},{3,1},{5,7},{10,8},{12,14},{11,9},{13,15},{18,16},{20,... | collective-permute-start | bytes 884744 | tf_op jit(solution)/shard_map/ppermute | solution.py:30
  86.5 69.4 %collective-permute-start.16 = (bf16[64,4608]{1,0:T(8,128)(2,1)}, bf16[64,4608]{1,0:T(8,128)(2,1)}, u32[]{:S(2)}, u32[]{:S(2)}) collective-permute-start(bf16[64,4608]{1,0:T(8,128)(2,1)} %get-tuple-element.59.refs_0_), channel_id=1, source_target_pairs={{2,4},{4,2},{3,5},{5,3},{10,12},{12,10},{11,13},{13,11},{18,20},{2... | collective-permute-start | bytes 1769480 | tf_op jit(solution)/shard_map/ppermute | solution.py:24
  88.0 80.6 %collective-permute-start.1 = (bf16[64,4608]{1,0:T(8,128)(2,1)S(1)}, bf16[64,4608]{1,0:T(8,128)(2,1)}, u32[]{:S(2)}, u32[]{:S(2)}) collective-permute-start(bf16[64,4608]{1,0:T(8,128)(2,1)S(1)} %get-tuple-element.47.refs_0_), channel_id=1, source_target_pairs={{0,4},{2,6},{4,0},{6,2},{1,5},{3,7},{5,1},{7,3},{8,12},{10,14},{12... | collective-permute-start | bytes 1769480 | tf_op jit(solution)/shard_map/ppermute | solution.py:16
  136.9 27.7 %collective-permute-start.8 = (bf16[64,4608]{1,0:T(8,128)(2,1)}, bf16[64,4608]{1,0:T(8,128)(2,1)}, u32[]{:S(2)}, u32[]{:S(2)}) collective-permute-start(bf16[64,4608]{1,0:T(8,128)(2,1)} %get-tuple-element.54.refs_0_), channel_id=1, source_target_pairs={{0,4},{2,6},{4,0},{6,2},{1,5},{3,7},{5,1},{7,3},{8,12},{10,14},{12... | collective-permute-start | bytes 1769480 | tf_op jit(solution)/shard_map/ppermute | solution.py:16
  145.8 30.9 %collective-permute-start.17 = (bf16[64,4608]{1,0:T(8,128)(2,1)}, bf16[64,4608]{1,0:T(8,128)(2,1)}, u32[]{:S(2)}, u32[]{:S(2)}) collective-permute-start(bf16[64,4608]{1,0:T(8,128)(2,1)} %collective-permute-done.15.refs_2_), channel_id=1, source_target_pairs={{2,0},{4,6},{3,1},{5,7},{10,8},{12,14},{11,9},{13,15},{18,16},{20,... | collective-permute-start | bytes 1769480 | tf_op jit(solution)/shard_map/ppermute | solution.py:30
  152.4 37.0 %collective-permute-start.7 = (bf16[64,4608]{1,0:T(8,128)(2,1)}, bf16[64,4608]{1,0:T(8,128)(2,1)}, u32[]{:S(2)}, u32[]{:S(2)}) collective-permute-start(bf16[64,4608]{1,0:T(8,128)(2,1)} %get-tuple-element.54.refs_0_), channel_id=1, source_target_pairs={{0,2},{2,0},{4,6},{6,4},{1,3},{3,1},{5,7},{7,5},{8,10},{10,8},{12,... | collective-permute-start | bytes 1769480 | tf_op jit(solution)/shard_map/ppermute | solution.py:16
  155.9 34.9 %collective-permute-start.9 = (bf16[64,4608]{1,0:T(8,128)(2,1)}, bf16[64,4608]{1,0:T(8,128)(2,1)}, u32[]{:S(2)}, u32[]{:S(2)}) collective-permute-start(bf16[64,4608]{1,0:T(8,128)(2,1)} %get-tuple-element.54.refs_0_), channel_id=1, source_target_pairs={{2,4},{4,2},{3,5},{5,3},{10,12},{12,10},{11,13},{13,11},{18,20},{2... | collective-permute-start | bytes 1769480 | tf_op jit(solution)/shard_map/ppermute | solution.py:24
  164.6 37.4 %collective-permute-start.10 = (bf16[64,4608]{1,0:T(8,128)(2,1)}, bf16[64,4608]{1,0:T(8,128)(2,1)}, u32[]{:S(2)}, u32[]{:S(2)}) collective-permute-start(bf16[64,4608]{1,0:T(8,128)(2,1)} %collective-permute-done.8.refs_2_), channel_id=1, source_target_pairs={{2,0},{4,6},{3,1},{5,7},{10,8},{12,14},{11,9},{13,15},{18,16},{20,... | collective-permute-start | bytes 1769480 | tf_op jit(solution)/shard_map/ppermute | solution.py:30
  168.6 41.0 %collective-permute-start.2 = (bf16[64,4608]{1,0:T(8,128)(2,1)S(1)}, bf16[64,4608]{1,0:T(8,128)(2,1)}, u32[]{:S(2)}, u32[]{:S(2)}) collective-permute-start(bf16[64,4608]{1,0:T(8,128)(2,1)S(1)} %get-tuple-element.47.refs_0_), channel_id=1, source_target_pairs={{2,4},{4,2},{3,5},{5,3},{10,12},{12,10},{11,13},{13,11},{18,20},{2... | collective-permute-start | bytes 1769480 | tf_op jit(solution)/shard_map/ppermute | solution.py:24
  176.7 36.8 %collective-permute-start.3 = (bf16[64,4608]{1,0:T(8,128)(2,1)}, bf16[64,4608]{1,0:T(8,128)(2,1)}, u32[]{:S(2)}, u32[]{:S(2)}) collective-permute-start(bf16[64,4608]{1,0:T(8,128)(2,1)} %collective-permute-done.1.refs_2_), channel_id=1, source_target_pairs={{2,0},{4,6},{3,1},{5,7},{10,8},{12,14},{11,9},{13,15},{18,16},{20,... | collective-permute-start | bytes 1769480 | tf_op jit(solution)/shard_map/ppermute | solution.py:30
  189.4 114.6 %collective-permute-start.21 = (bf16[576,4608]{1,0:T(8,128)(2,1)}, bf16[576,4608]{1,0:T(8,128)(2,1)}, u32[]{:S(2)}, u32[]{:S(2)}) collective-permute-start(bf16[576,4608]{1,0:T(8,128)(2,1)} %fusion.1), channel_id=1, source_target_pairs={{0,1},{1,0},{2,3},{3,2},{4,5},{5,4},{6,7},{7,6},{8,9},{9,8},{10,11... | collective-permute-start | bytes 15925256 | tf_op jit(solution)/shard_map/ppermute | solution.py:16
  190.8 29.1 %collective-permute-start.18 = (bf16[64,4608]{1,0:T(8,128)(2,1)}, bf16[64,4608]{1,0:T(8,128)(2,1)}, u32[]{:S(2)}, u32[]{:S(2)}) collective-permute-start(bf16[64,4608]{1,0:T(8,128)(2,1)} %get-tuple-element.61), channel_id=1, source_target_pairs={{0,8},{8,0},{16,24},{24,16},{1,9},{9,1},{17,25},{25,17},{2,10},{10... | collective-permute-start | bytes 1769480 | tf_op jit(solution)/shard_map/ppermute | solution.py:16
  223.0 31.6 %collective-permute-start.13 = (bf16[64,4608]{1,0:T(8,128)(2,1)S(1)}, bf16[64,4608]{1,0:T(8,128)(2,1)S(1)}, u32[]{:S(2)}, u32[]{:S(2)}) collective-permute-start(bf16[64,4608]{1,0:T(8,128)(2,1)S(1)} %copy-done.37), channel_id=1, source_target_pairs={{0,24},{8,16},{16,8},{24,0},{1,25},{9,17},{17,9},{25,1},{2,26},{10... | collective-permute-start | bytes 1769480 | tf_op jit(solution)/shard_map/ppermute | solution.py:16
  232.8 35.8 %collective-permute-start.5 = (bf16[64,4608]{1,0:T(8,128)(2,1)S(1)}, bf16[64,4608]{1,0:T(8,128)(2,1)S(1)}, u32[]{:S(2)}, u32[]{:S(2)}) collective-permute-start(bf16[64,4608]{1,0:T(8,128)(2,1)S(1)} %copy-done.39), channel_id=1, source_target_pairs={{0,16},{8,24},{16,0},{24,8},{1,17},{9,25},{17,1},{25,9},{2,18},{10... | collective-permute-start | bytes 1769480 | tf_op jit(solution)/shard_map/ppermute | solution.py:16
  243.3 34.4 %collective-permute-start.6 = (bf16[64,4608]{1,0:T(8,128)(2,1)S(1)}, bf16[64,4608]{1,0:T(8,128)(2,1)S(1)}, u32[]{:S(2)}, u32[]{:S(2)}) collective-permute-start(bf16[64,4608]{1,0:T(8,128)(2,1)S(1)} %copy-done.38), channel_id=1, source_target_pairs={{0,24},{8,16},{16,8},{24,0},{1,25},{9,17},{17,9},{25,1},{2,26},{10... | collective-permute-start | bytes 1769480 | tf_op jit(solution)/shard_map/ppermute | solution.py:16
  392.7 52.9 %collective-permute-start.57 = (bf16[64,576]{1,0:T(8,128)(2,1)S(1)}, bf16[64,576]{1,0:T(8,128)(2,1)}, u32[]{:S(2)}, u32[]{:S(2)}) collective-permute-start(bf16[64,576]{1,0:T(8,128)(2,1)S(1)} %get-tuple-element.93.refs_0_), channel_id=1, source_target_pairs={{0,16},{8,24},{16,0},{24,8},{1,17},{9,25},{17,1},{25,9},{2,18},{10... | collective-permute-start | bytes 221192 | tf_op jit(solution)/shard_map/ppermute | solution.py:16
  399.7 47.5 %collective-permute-start.58 = (bf16[64,576]{1,0:T(8,128)(2,1)S(1)}, bf16[64,576]{1,0:T(8,128)(2,1)}, u32[]{:S(2)}, u32[]{:S(2)}) collective-permute-start(bf16[64,576]{1,0:T(8,128)(2,1)S(1)} %get-tuple-element.93.refs_0_), channel_id=1, source_target_pairs={{0,24},{8,16},{16,8},{24,0},{1,25},{9,17},{17,9},{25,1},{2,26},{10... | collective-permute-start | bytes 221192 | tf_op jit(solution)/shard_map/ppermute | solution.py:16
  436.6 35.6 %collective-permute-start.62 = (bf16[768,576]{0,1:T(8,128)(2,1)S(1)}, bf16[768,576]{0,1:T(8,128)(2,1)S(1)}, u32[]{:S(2)}, u32[]{:S(2)}) collective-permute-start(bf16[768,576]{0,1:T(8,128)(2,1)S(1)} %copy.35), channel_id=1, source_target_pairs={{0,1},{1,0},{2,3},{3,2},{4,5},{5,4},{6,7},{7,6},{8,9},{9,8},{10,11... | collective-permute-start | bytes 2654216 | tf_op jit(solution)/shard_map/ppermute | solution.py:16
  (92 other events, 1574.8 us)
where the time goes:
time: 484 us; the launch traced here: 482 us
  waiting for transfers between devices  251 us (52%)
  starting transfers between devices  79.6 us (16%)
  matrix products  44.7 us (9%)
  Pallas kernels  38.4 us (8%)
  local copies, waits for them, and re-layouts  35.6 us (7%)
  other arithmetic  31 us (6%)
    ppermute x53, waiting for transfers between devices, swap(): lax.ppermute(value, axis, [(i, i ^ offset) for i in range(lax.axis_size(a...  222 us
    ppermute x53, starting transfers between devices, swap(): lax.ppermute(value, axis, [(i, i ^ offset) for i in range(lax.axis_size(a...  63.1 us
    dot_general x10, matrix products, contract_last(): lax.dot_general(left, right, (((1,), (1,)), ((), ())), preferred_element_...  39.9 us
    pallas_call x11, Pallas kernels, xor_order(): pl.pallas_call(functools.partial(order_kernel, size), grid_spec=pltpu.Pre...  38.4 us
    ppermute x7, waiting for transfers between devices, spread_last(): return list(blocks) + [lax.ppermute(blocks[2], axis, [(1, 0), (2, 3)])]  29.4 us
    unnamed x124, local copies, waits for them, and re-layouts  21.3 us
    mul x2, other arithmetic, pruned(): w * lax.dynamic_slice(mask, (0, block * depth), (cols, depth)).astype(w.d...  19 us
  transfers between devices with their start and end apart: 67, of which 33 were waited for; matrix products, arithmetic and copies ran while one was open for 17% of the time, Pallas kernels for 7%

commit v1 on v0

--- a/solution.py
+++ b/solution.py
@@ -35,36 +35,93 @@
 
 
 def order_kernel(size, by_ref, *refs):
-    outs = refs[len(refs) - size :]
-    blocks = refs[: len(refs) - size]
-
-    def write(by, last):
-        for k in range(size):
-            at = k ^ by
-            outs[k][...] = blocks[last if at == size - 1 else at][...]
-
-    for by in range(size):
-        if len(blocks) == size:
-            pl.when(by_ref[0] == by)(functools.partial(write, by, size - 1))
-        else:
-            for end in range(2):
-                pl.when((by_ref[0] == by) & (by_ref[1] == end))(functools.partial(write, by, size - 1 + end))
+    outs, (held, in_sems, out_sems) = refs[-size - 3 : -3], refs[-3:]
+    blocks = refs[: -size - 3]
+    for k in range(size):
+        at = k ^ by_ref[0]
+        at = jnp.where((at == size - 1) & (by_ref[1] == 1), len(blocks) - 1, at)
+        for b, block in enumerate(blocks):
+            pl.when(at == b)(pltpu.make_async_copy(block, held.at[k], in_sems.at[k]).start)
+    for k in range(size):
+        pltpu.make_async_copy(blocks[0], held.at[k], in_sems.at[k]).wait()
+        pltpu.make_async_copy(held.at[k], outs[k], out_sems.at[k]).start()
+    for k in range(size):
+        pltpu.make_async_copy(held.at[k], outs[k], out_sems.at[k]).wait()
 
 
 def xor_order(blocks, by, axis):
     size, index = lax.axis_size(axis), lax.axis_index(axis)
     at_end = (index == 0) | (index == size - 1)
     rows, cols = blocks[0].shape
-    tile = 16 if rows % 16 == 0 and cols >= 2048 else rows
-    spec = pl.BlockSpec((tile, cols), lambda i, by: (i, 0))
+    dtype = blocks[0].dtype
+    hbm = pl.BlockSpec(memory_space=pltpu.HBM)
     return pl.pallas_call(
         functools.partial(order_kernel, size),
-        grid_spec=pltpu.PrefetchScalarGridSpec(
-            num_scalar_prefetch=1, grid=(rows // tile,), in_specs=[spec] * len(blocks), out_specs=[spec] * size
+        in_specs=[pl.BlockSpec(memory_space=pltpu.SMEM)] + [hbm] * len(blocks),
+        out_specs=[hbm] * size,
+        out_shape=[jax.ShapeDtypeStruct((rows, cols), dtype)] * size,
+        scratch_shapes=[pltpu.VMEM((size, rows, cols), dtype), pltpu.SemaphoreType.DMA((size,)), pltpu.SemaphoreType.DMA((size,))],
+        cost_estimate=pl.CostEstimate(flops=rows * cols * size, bytes_accessed=4 * rows * cols * size, transcendentals=0),
+        name="order",
+    )(jnp.stack([by, at_end.astype(jnp.int32)]), *blocks)
+
+
+def product_kernel(toks, subs, chunks, *refs):
+    lefts, weights = refs[: toks * chunks], refs[toks * chunks : toks * chunks + subs]
+    keep, send, total = refs[toks * chunks + subs :]
+    step = pl.program_id(0)
+    left = jnp.concatenate([ref[...] for ref in lefts], axis=0)
+    n = left.shape[0] // toks
+    for k in range(subs):
+        term = contract_last(left, weights[k][...])
+
+        @pl.when(step == 0)
+        def _(k=k, term=term):
+            total[k] = term
+
+        @pl.when(step > 0)
+        def _(k=k, term=term):
+            total[k] += term
+
+    @pl.when(step == pl.num_programs(0) - 1)
+    def _():
+        for k in range(subs):
+            for d in range(0, toks, 2):
+                keep[k, d // 2] = total[k, d * n : (d + 1) * n]
+                send[k, d // 2] = total[k, (d + 1) * n : (d + 2) * n].astype(send.dtype)
+
+
+def product(lefts, weights):
+    toks, chunks, subs = len(lefts), len(lefts[0]), len(weights)
+    n = sum(piece.shape[0] for piece in lefts[0])
+    cols, depth = weights[0].shape
+    tile = depth // 4 if depth % 512 == 0 else depth
+    flat = [piece for pieces in lefts for piece in pieces]
+    shape = (subs, toks // 2, n, cols)
+    whole = pl.BlockSpec(shape, lambda i: (0, 0, 0, 0))
+    return pl.pallas_call(
+        functools.partial(product_kernel, toks, subs, chunks),
+        grid=(depth // tile,),
+        in_specs=[pl.BlockSpec((piece.shape[0], tile), lambda i: (0, i)) for piece in flat]
+        + [pl.BlockSpec((cols, tile), lambda i: (0, i))] * subs,
+        out_specs=[whole, whole],
+        out_shape=[jax.ShapeDtypeStruct(shape, jnp.float32), jax.ShapeDtypeStruct(shape, jnp.bfloat16)],
+        scratch_shapes=[pltpu.VMEM((subs, toks * n, cols), jnp.float32)],
+        cost_estimate=pl.CostEstimate(
+            flops=2 * toks * n * cols * depth * subs, bytes_accessed=2 * depth * (toks * n + cols * subs), transcendentals=0
         ),
-        out_shape=[jax.ShapeDtypeStruct((rows, cols), blocks[0].dtype)] * size,
-        cost_estimate=pl.CostEstimate(flops=rows * cols * size, bytes_accessed=4 * rows * cols * size, transcendentals=0),
-    )(jnp.stack([by, at_end.astype(jnp.int32)]), *blocks)
+        name="product",
+    )(*flat, *weights)
+
+
+def select_order(blocks, by):
+    size = len(blocks)
+    bit = 1
+    while bit < size:
+        flip = jnp.broadcast_to((by & bit) != 0, blocks[0].shape)
+        blocks = [lax.select(flip, blocks[k ^ bit], blocks[k]) for k in range(size)]
+        bit *= 2
+    return blocks
 
 
 def turn(blocks, axis):
@@ -99,34 +156,31 @@
     weight, mask, _ = lax.optimization_barrier((down_weight, keep_mask, seen[0][1]))
     weights = [pruned(weight, mask, sub)] + sent
 
-    shares = [[] for _ in range(subs)]
+    arrived = []
     for j in range(len(steps)):
         blocks = spread_last(seen[j], "row")
-        chunk = jnp.concatenate(turn(xor_order(blocks, tok ^ row, "row"), "tok"), axis=0)
-        for k in range(subs):
-            shares[k].append(contract_last(chunk, weights[k]))
+        arrived.append(turn(xor_order(blocks, tok ^ row, "row"), "tok"))
 
     left, right, layer_rows = [], [], []
     for group in GROUPS:
-
-        def take(k):
-            parts = [shares[k][j].reshape(toks, steps[j], cols) for j in group]
-            return jnp.concatenate(parts, axis=1) if len(parts) > 1 else parts[0]
-
-        total = take(0)
+        keep, send = product([[arrived[j][d] for j in group] for d in range(toks)], weights)
+        total = keep + swap(send, "tok", 1).astype(jnp.float32)
+        rest = total[1:].astype(small)
+        total = total[0]
         for k in range(1, subs):
-            total = total + swap(take(k).astype(small), "sub", k).astype(jnp.float32)
-        rest = total[1:].astype(small)
-        layer = total[0]
-        for k in range(1, toks):
-            layer = layer + swap(rest[k - 1], "tok", k).astype(jnp.float32)
-        layer = layer.astype(small)
+            total = total + swap(rest[k - 1], "sub", k).astype(jnp.float32)
+        bit = 2
+        while bit < toks:
+            total = total.reshape((-1, 2) + total.shape[1:])
+            total = total[:, 0] + swap(total[:, 1].astype(small), "tok", bit).astype(jnp.float32)
+            bit *= 2
+        layer = total[0].astype(small)
         blocks = spread(layer, "row")
         left.append(jnp.concatenate(turn([layer] * toks, "tok"), axis=0))
         layer_rows.append(blocks)
         mine = jnp.concatenate(turn(xor_order(blocks, tok ^ row, "row"), "tok"), axis=0)
         both = [mine] + [swap(mine, "sub", k) for k in range(1, subs)]
-        right.append(jnp.concatenate(xor_order(both, sub, "sub"), axis=1))
+        right.append(jnp.concatenate(select_order(both, sub), axis=1))
 
     scaling = 2.0 / (rows * toks)
     hessian = contract_rows(jnp.concatenate(left, axis=0), jnp.concatenate(right, axis=0)) * scaling
@@ -139,7 +193,7 @@
         return lax.dynamic_slice(whole, (0, row, other, 0, 0), (toks, 1, 1, share, cols)).reshape(toks * share, cols)
 
     pieces = [for_sub(sub)] + [swap(for_sub(sub ^ k), "sub", k) for k in range(1, subs)]
-    pieces = [piece.reshape(toks, share, cols) for piece in xor_order(pieces, sub, "sub")]
+    pieces = [piece.reshape(toks, share, cols) for piece in select_order(pieces, sub)]
     layer_out = jnp.stack(pieces, axis=1).transpose(2, 0, 1, 3).reshape(share, toks * subs * cols)
     return layer_out, hessian
 

time: 484 us -> 446 us (0.921)
  matrix products: 44.7 us -> 3.31 us
  local copies, waits for them, and re-layouts: 35.6 us -> 11.6 us
  Pallas kernels: 38.4 us -> 55.8 us
  starting transfers between devices: 79.6 us -> 94.4 us
    dot_general x10 -> x0, matrix products: 39.9 us -> none  [contract_last(): lax.dot_general(left, right, (((1,), (1,)), ((), ())), preferred_element_...]
    pallas_call x11 -> x10, Pallas kernels: 38.4 us -> 55.8 us  [the longest x2 32.6 us: product(): pl.pallas_call(functools.partial(product_kernel, toks, subs, chunks), gri...]
    ppermute x53 -> x51, starting transfers between devices: 63.1 us -> 79.4 us  [swap(): lax.ppermute(value, axis, [(i, i ^ offset) for i in range(lax.axis_size(a...]
    unnamed x124 -> x111, local copies, waits for them, and re-layouts: 21.3 us -> 7.91 us
    ppermute x53 -> x51, waiting for transfers between devices: 222 us -> 222 us  [swap(): lax.ppermute(value, axis, [(i, i ^ offset) for i in range(lax.axis_size(a...]
  transfers between devices with their start and end apart: 67 -> 65, of which waited for: 33 -> 27; matrix products, arithmetic and copies ran while one was open for 17% -> 5% of each run, Pallas kernels for 7% -> 13%
where the time goes in v1:
time: 446 us; the launch traced here: 445 us
  waiting for transfers between devices  251 us (56%)
  starting transfers between devices  94.4 us (21%)
  Pallas kernels  55.8 us (13%)
  other arithmetic  28.4 us (6%)
  local copies, waits for them, and re-layouts  11.6 us (3%)
    ppermute x51, waiting for transfers between devices, swap(): lax.ppermute(value, axis, [(i, i ^ offset) for i in range(lax.axis_size(a...  222 us
    ppermute x51, starting transfers between devices, swap(): lax.ppermute(value, axis, [(i, i ^ offset) for i in range(lax.axis_size(a...  79.4 us
    pallas_call x2, Pallas kernels, product(): pl.pallas_call(functools.partial(product_kernel, toks, subs, chunks), gri...  32.6 us
    ppermute x7, waiting for transfers between devices, spread_last(): return list(blocks) + [lax.ppermute(blocks[2], axis, [(1, 0), (2, 3)])]  28.9 us
    pallas_call x8, Pallas kernels, xor_order(): pl.pallas_call(functools.partial(order_kernel, size), in_specs=[pl.BlockS...  23.2 us
    mul x2, other arithmetic, pruned(): w * lax.dynamic_slice(mask, (0, block * depth), (cols, depth)).astype(w.d...  19.3 us
    ppermute x7, starting transfers between devices, spread_last(): return list(blocks) + [lax.ppermute(blocks[2], axis, [(1, 0), (2, 3)])]  9.41 us
  transfers between devices with their start and end apart: 65, of which 27 were waited for; matrix products, arithmetic and copies ran while one was open for 5% of the time, Pallas kernels for 13%

profile of v1, /device:TPU:0, one launch (start us, length us, event | category | flops | bytes accessed | tf_op | source)
XLA Modules:
  0.0 445.4 jit_solution(5674103451684289552)
XLA Ops:
  0.7 9.6 %fusion.1 = bf16[576,4608]{1,0:T(8,128)(2,1)} fusion(s32[576,9216]{1,0:T(8,128)} %param.5, s32[]{:T(128)S(6)} %select_n.37, bf16[576,9216]{1,0:T(8,128)(2,1)} %param.4), kind=kLoop, calls=%fused_computation.3 | loop fusion | flops 13271040 | bytes 21233668 | tf_op jit(solution)/shard_map/mul | solution.py:150
  20.6 41.3 %collective-permute-done.26.refs_2_ = bf16[32,4608]{1,0:T(8,128)(2,1)S(1)} collective-permute-done((bf16[32,4608]{1,0:T(8,128)(2,1)S(1)}, bf16[32,4608]{1,0:T(8,128)(2,1)S(1)}, u32[]{:S(2)}, u32[]{:S(2)}) %collective-permute-start.26) | collective-permute-done | bytes 294944 | tf_op jit(solution)/shard_map/ppermute | solution.py:16
  68.1 11.7 %collective-permute-done.refs_1_ = bf16[64,4608]{1,0:T(8,128)(2,1)S(1)} collective-permute-done((bf16[64,4608]{1,0:T(8,128)(2,1)S(1)}, bf16[64,4608]{1,0:T(8,128)(2,1)S(1)}, u32[]{:S(2)}, u32[]{:S(2)}) %collective-permute-start) | collective-permute-done | bytes 589856 | tf_op jit(solution)/shard_map/ppermute | solution.py:16
  81.1 25.7 %collective-permute-done.9.refs_2_ = bf16[64,4608]{1,0:T(8,128)(2,1)S(1)} collective-permute-done((bf16[64,4608]{1,0:T(8,128)(2,1)S(1)}, bf16[64,4608]{1,0:T(8,128)(2,1)S(1)}, u32[]{:S(2)}, u32[]{:S(2)}) %collective-permute-start.9) | collective-permute-done | bytes 589856 | tf_op jit(solution)/shard_map/ppermute | solution.py:16
  108.8 26.6 %collective-permute-start.4 = (bf16[64,4608]{1,0:T(8,128)(2,1)S(1)}, bf16[64,4608]{1,0:T(8,128)(2,1)}, u32[]{:S(2)}, u32[]{:S(2)}) collective-permute-start(bf16[64,4608]{1,0:T(8,128)(2,1)S(1)} %get-tuple-element.47.refs_0_), channel_id=1, source_target_pairs={{0,2},{2,0},{4,6},{6,4},{1,3},{3,1},{5,7},{7,5},{8,10},{10,8},{12,... | collective-permute-start | bytes 1769480 | tf_op jit(solution)/shard_map/ppermute | solution.py:16
  146.0 10.0 %collective-permute-done.11.refs_4_ = bf16[64,4608]{1,0:T(8,128)(2,1)} collective-permute-done((bf16[64,4608]{1,0:T(8,128)(2,1)S(1)}, bf16[64,4608]{1,0:T(8,128)(2,1)}, u32[]{:S(2)}, u32[]{:S(2)}) %collective-permute-start.11) | collective-permute-done | bytes 589856 | tf_op jit(solution)/shard_map/ppermute | solution.py:30
  159.3 9.4 %collective-permute-done.4.refs_1_ = bf16[64,4608]{1,0:T(8,128)(2,1)} collective-permute-done((bf16[64,4608]{1,0:T(8,128)(2,1)S(1)}, bf16[64,4608]{1,0:T(8,128)(2,1)}, u32[]{:S(2)}, u32[]{:S(2)}) %collective-permute-start.4) | collective-permute-done | bytes 589856 | tf_op jit(solution)/shard_map/ppermute | solution.py:16
  170.2 10.9 %collective-permute-done.7.refs_4_ = bf16[64,4608]{1,0:T(8,128)(2,1)S(1)} collective-permute-done((bf16[64,4608]{1,0:T(8,128)(2,1)S(1)}, bf16[64,4608]{1,0:T(8,128)(2,1)S(1)}, u32[]{:S(2)}, u32[]{:S(2)}) %collective-permute-start.7) | collective-permute-done | bytes 589856 | tf_op jit(solution)/shard_map/ppermute | solution.py:30
  186.4 10.4 %collective-permute-done.18.refs_9_ = bf16[64,4608]{1,0:T(8,128)(2,1)S(1)} collective-permute-done((bf16[64,4608]{1,0:T(8,128)(2,1)}, bf16[64,4608]{1,0:T(8,128)(2,1)S(1)}, u32[]{:S(2)}, u32[]{:S(2)}) %collective-permute-start.18) | collective-permute-done | bytes 589856 | tf_op jit(solution)/shard_map/ppermute | solution.py:16
  199.1 11.3 %collective-permute-done.17.refs_8_ = bf16[64,4608]{1,0:T(8,128)(2,1)S(1)} collective-permute-done((bf16[64,4608]{1,0:T(8,128)(2,1)}, bf16[64,4608]{1,0:T(8,128)(2,1)S(1)}, u32[]{:S(2)}, u32[]{:S(2)}) %collective-permute-start.17) | collective-permute-done | bytes 589856 | tf_op jit(solution)/shard_map/ppermute | solution.py:16
  210.5 9.7 %fusion.refs_12_.refs_8_ = bf16[576,4608]{1,0:T(8,128)(2,1)} fusion(s32[576,9216]{1,0:T(8,128)} %param.5, s32[]{:T(128)S(6)} %select_n.36, bf16[576,9216]{1,0:T(8,128)(2,1)} %param.4), kind=kLoop, calls=%fused_computation.2 | loop fusion | flops 13271040 | bytes 21233668 | tf_op jit(solution)/shard_map/mul | solution.py:150
  226.0 9.8 %collective-permute-done.16.refs_7_ = bf16[64,4608]{1,0:T(8,128)(2,1)} collective-permute-done((bf16[64,4608]{1,0:T(8,128)(2,1)}, bf16[64,4608]{1,0:T(8,128)(2,1)}, u32[]{:S(2)}, u32[]{:S(2)}) %collective-permute-start.16) | collective-permute-done | bytes 589856 | tf_op jit(solution)/shard_map/ppermute | solution.py:16
  236.4 9.9 %collective-permute-done.19.refs_10_ = bf16[64,4608]{1,0:T(8,128)(2,1)} collective-permute-done((bf16[64,4608]{1,0:T(8,128)(2,1)}, bf16[64,4608]{1,0:T(8,128)(2,1)}, u32[]{:S(2)}, u32[]{:S(2)}) %collective-permute-start.19) | collective-permute-done | bytes 589856 | tf_op jit(solution)/shard_map/ppermute | solution.py:16
  249.2 22.0 %product.2 = (f32[2,2,192,576]{3,2,1,0:T(8,128)}, bf16[2,2,192,576]{3,2,1,0:T(8,128)(2,1)}) custom-call(bf16[64,4608]{1,0:T(8,128)(2,1)} %get-tuple-element.46.refs_0_, bf16[64,4608]{1,0:T(8,128)(2,1)} %get-tuple-element.48.refs_1_, bf16[64,4608]{1,0:T(8,128)(2,1)} %get-tuple-element.50.refs_2_, bf16[64,4608]{1,0:T(8,128)(2,1)} %collective-permute-done.12.refs_3_, ...), custom_call_target="tpu_custom_call" | custom-call | flops 8153726976 | bytes 17694720 | tf_op jit(solution)/shard_map/product/pallas_call | solution.py:102
  285.1 5.7 %collective-permute-done.35.refs_4_ = bf16[32,4608]{1,0:T(8,128)(2,1)S(1)} collective-permute-done((bf16[32,4608]{1,0:T(8,128)(2,1)}, bf16[32,4608]{1,0:T(8,128)(2,1)S(1)}, u32[]{:S(2)}, u32[]{:S(2)}) %collective-permute-start.35) | collective-permute-done | bytes 294944 | tf_op jit(solution)/shard_map/ppermute | solution.py:16
  290.8 6.3 %collective-permute-done.36.refs_5_ = bf16[32,4608]{1,0:T(8,128)(2,1)S(1)} collective-permute-done((bf16[32,4608]{1,0:T(8,128)(2,1)}, bf16[32,4608]{1,0:T(8,128)(2,1)S(1)}, u32[]{:S(2)}, u32[]{:S(2)}) %collective-permute-start.36) | collective-permute-done | bytes 294944 | tf_op jit(solution)/shard_map/ppermute | solution.py:16
  297.1 5.4 %collective-permute-done.37.refs_6_ = bf16[32,4608]{1,0:T(8,128)(2,1)S(1)} collective-permute-done((bf16[32,4608]{1,0:T(8,128)(2,1)}, bf16[32,4608]{1,0:T(8,128)(2,1)S(1)}, u32[]{:S(2)}, u32[]{:S(2)}) %collective-permute-start.37) | collective-permute-done | bytes 294944 | tf_op jit(solution)/shard_map/ppermute | solution.py:16
  302.6 6.1 %collective-permute-done.38.refs_7_ = bf16[32,4608]{1,0:T(8,128)(2,1)S(1)} collective-permute-done((bf16[32,4608]{1,0:T(8,128)(2,1)}, bf16[32,4608]{1,0:T(8,128)(2,1)S(1)}, u32[]{:S(2)}, u32[]{:S(2)}) %collective-permute-start.38) | collective-permute-done | bytes 294944 | tf_op jit(solution)/shard_map/ppermute | solution.py:16
  309.4 10.6 %product.3 = (f32[2,2,64,576]{3,2,1,0:T(8,128)}, bf16[2,2,64,576]{3,2,1,0:T(8,128)(2,1)}) custom-call(bf16[32,4608]{1,0:T(8,128)(2,1)} %get-tuple-element.65.refs_0_, bf16[32,4608]{1,0:T(8,128)(2,1)} %get-tuple-element.67.refs_1_, bf16[32,4608]{1,0:T(8,128)(2,1)} %copy-done.28, bf16[32,4608]{1,0:T(8,128)(2,1)} %copy-done.29, bf16[32,4608]{1,0:T(8,128)(2,1)} %copy-done.30, ...), custom_call_target="tpu_custom_call" | custom-call | flops 2717908992 | bytes 12976128 | tf_op jit(solution)/shard_map/product/pallas_call | solution.py:102
  322.8 11.9 %collective-permute-done.23 = bf16[2,192,576]{2,1,0:T(8,128)(2,1)S(1)} collective-permute-done((bf16[2,192,576]{2,1,0:T(8,128)(2,1)S(1)}, bf16[2,192,576]{2,1,0:T(8,128)(2,1)S(1)}, u32[]{:S(2)}, u32[]{:S(2)}) %collective-permute-start.23) | collective-permute-done | bytes 442400 | tf_op jit(solution)/shard_map/ppermute | solution.py:16
  351.1 5.2 %collective-permute-done.53 = bf16[192,576]{1,0:T(8,128)(2,1)S(1)} collective-permute-done((bf16[192,576]{1,0:T(8,128)(2,1)S(1)}, bf16[192,576]{1,0:T(8,128)(2,1)S(1)}, u32[]{:S(2)}, u32[]{:S(2)}) %collective-permute-start.53) | collective-permute-done | bytes 221216 | tf_op jit(solution)/shard_map/ppermute | solution.py:16
  375.2 7.9 %collective-permute-done.49.refs_4_ = bf16[64,576]{1,0:T(8,128)(2,1)S(1)} collective-permute-done((bf16[64,576]{1,0:T(8,128)(2,1)S(1)}, bf16[64,576]{1,0:T(8,128)(2,1)S(1)}, u32[]{:S(2)}, u32[]{:S(2)}) %collective-permute-start.49) | collective-permute-done | bytes 73760 | tf_op jit(solution)/shard_map/ppermute | solution.py:30
  401.6 7.3 %collective-permute-done.59 = bf16[192,576]{1,0:T(8,128)(2,1)S(1)} collective-permute-done((bf16[192,576]{1,0:T(8,128)(2,1)S(1)}, bf16[192,576]{1,0:T(8,128)(2,1)S(1)}, u32[]{:S(2)}, u32[]{:S(2)}) %collective-permute-start.59) | collective-permute-done | bytes 221216 | tf_op jit(solution)/shard_map/ppermute | solution.py:16
  413.9 25.3 %collective-permute-done.64 = bf16[256,576]{1,0:T(8,128)(2,1)S(1)} collective-permute-done((bf16[256,576]{1,0:T(8,128)(2,1)S(1)}, bf16[256,576]{1,0:T(8,128)(2,1)S(1)}, u32[]{:S(2)}, u32[]{:S(2)}) %collective-permute-start.64) | collective-permute-done | bytes 294944 | tf_op jit(solution)/shard_map/ppermute | solution.py:16
  (262 shorter events, 133.7 us)
Async XLA Ops:
  10.2 237.4 %collective-permute-start.21 = (bf16[576,4608]{1,0:T(8,128)(2,1)}, bf16[576,4608]{1,0:T(8,128)(2,1)}, u32[]{:S(2)}, u32[]{:S(2)}) collective-permute-start(bf16[576,4608]{1,0:T(8,128)(2,1)} %fusion.1), channel_id=1, source_target_pairs={{0,1},{1,0},{2,3},{3,2},{4,5},{5,4},{6,7},{7,6},{8,9},{9,8},{10,11... | collective-permute-start | bytes 15925256 | tf_op jit(solution)/shard_map/ppermute | solution.py:16
  13.4 54.0 %collective-permute-start.1 = (bf16[64,4608]{1,0:T(8,128)(2,1)S(1)}, bf16[64,4608]{1,0:T(8,128)(2,1)S(1)}, u32[]{:S(2)}, u32[]{:S(2)}) collective-permute-start(bf16[64,4608]{1,0:T(8,128)(2,1)S(1)} %get-tuple-element.45.refs_0_), channel_id=1, source_target_pairs={{0,4},{2,6},{4,0},{6,2},{1,5},{3,7},{5,1},{7,3},{8,12},{10,14},{12... | collective-permute-start | bytes 1769480 | tf_op jit(solution)/shard_map/ppermute | solution.py:16
  16.1 45.8 %collective-permute-start.26 = (bf16[32,4608]{1,0:T(8,128)(2,1)S(1)}, bf16[32,4608]{1,0:T(8,128)(2,1)S(1)}, u32[]{:S(2)}, u32[]{:S(2)}) collective-permute-start(bf16[32,4608]{1,0:T(8,128)(2,1)S(1)} %get-tuple-element.64.refs_0_), channel_id=1, source_target_pairs={{0,4},{2,6},{4,0},{6,2},{1,5},{3,7},{5,1},{7,3},{8,12},{10,14},{12... | collective-permute-start | bytes 884744 | tf_op jit(solution)/shard_map/ppermute | solution.py:16
  16.4 45.5 %collective-permute-start.25 = (bf16[32,4608]{1,0:T(8,128)(2,1)S(1)}, bf16[32,4608]{1,0:T(8,128)(2,1)S(1)}, u32[]{:S(2)}, u32[]{:S(2)}) collective-permute-start(bf16[32,4608]{1,0:T(8,128)(2,1)S(1)} %get-tuple-element.64.refs_0_), channel_id=1, source_target_pairs={{0,2},{2,0},{4,6},{6,4},{1,3},{3,1},{5,7},{7,5},{8,10},{10,8},{12,... | collective-permute-start | bytes 884744 | tf_op jit(solution)/shard_map/ppermute | solution.py:16
  18.0 49.3 %collective-permute-start.30 = (bf16[32,4608]{1,0:T(8,128)(2,1)S(1)}, bf16[32,4608]{1,0:T(8,128)(2,1)}, u32[]{:S(2)}, u32[]{:S(2)}) collective-permute-start(bf16[32,4608]{1,0:T(8,128)(2,1)S(1)} %get-tuple-element.66.refs_0_), channel_id=1, source_target_pairs={{0,4},{2,6},{4,0},{6,2},{1,5},{3,7},{5,1},{7,3},{8,12},{10,14},{12... | collective-permute-start | bytes 884744 | tf_op jit(solution)/shard_map/ppermute | solution.py:16
  67.3 39.5 %collective-permute-start.9 = (bf16[64,4608]{1,0:T(8,128)(2,1)S(1)}, bf16[64,4608]{1,0:T(8,128)(2,1)S(1)}, u32[]{:S(2)}, u32[]{:S(2)}) collective-permute-start(bf16[64,4608]{1,0:T(8,128)(2,1)S(1)} %get-tuple-element.49.refs_0_), channel_id=1, source_target_pairs={{0,4},{2,6},{4,0},{6,2},{1,5},{3,7},{5,1},{7,3},{8,12},{10,14},{12... | collective-permute-start | bytes 1769480 | tf_op jit(solution)/shard_map/ppermute | solution.py:16
  67.4 39.4 %collective-permute-start.10 = (bf16[64,4608]{1,0:T(8,128)(2,1)S(1)}, bf16[64,4608]{1,0:T(8,128)(2,1)S(1)}, u32[]{:S(2)}, u32[]{:S(2)}) collective-permute-start(bf16[64,4608]{1,0:T(8,128)(2,1)S(1)} %get-tuple-element.49.refs_0_), channel_id=1, source_target_pairs={{2,4},{4,2},{3,5},{5,3},{10,12},{12,10},{11,13},{13,11},{18,20},{2... | collective-permute-start | bytes 1769480 | tf_op jit(solution)/shard_map/ppermute | solution.py:24
  79.8 29.0 %collective-permute-start.8 = (bf16[64,4608]{1,0:T(8,128)(2,1)S(1)}, bf16[64,4608]{1,0:T(8,128)(2,1)}, u32[]{:S(2)}, u32[]{:S(2)}) collective-permute-start(bf16[64,4608]{1,0:T(8,128)(2,1)S(1)} %get-tuple-element.49.refs_0_), channel_id=1, source_target_pairs={{0,2},{2,0},{4,6},{6,4},{1,3},{3,1},{5,7},{7,5},{8,10},{10,8},{12,... | collective-permute-start | bytes 1769480 | tf_op jit(solution)/shard_map/ppermute | solution.py:16
  79.8 55.7 %collective-permute-start.3 = (bf16[64,4608]{1,0:T(8,128)(2,1)S(1)}, bf16[64,4608]{1,0:T(8,128)(2,1)}, u32[]{:S(2)}, u32[]{:S(2)}) collective-permute-start(bf16[64,4608]{1,0:T(8,128)(2,1)S(1)} %collective-permute-done.1.refs_2_), channel_id=1, source_target_pairs={{2,0},{4,6},{3,1},{5,7},{10,8},{12,14},{11,9},{13,15},{18,16},{20,... | collective-permute-start | bytes 1769480 | tf_op jit(solution)/shard_map/ppermute | solution.py:30
  106.8 38.0 %collective-permute-start.5 = (bf16[64,4608]{1,0:T(8,128)(2,1)S(1)}, bf16[64,4608]{1,0:T(8,128)(2,1)S(1)}, u32[]{:S(2)}, u32[]{:S(2)}) collective-permute-start(bf16[64,4608]{1,0:T(8,128)(2,1)S(1)} %get-tuple-element.47.refs_0_), channel_id=1, source_target_pairs={{0,4},{2,6},{4,0},{6,2},{1,5},{3,7},{5,1},{7,3},{8,12},{10,14},{12... | collective-permute-start | bytes 1769480 | tf_op jit(solution)/shard_map/ppermute | solution.py:16
  106.8 49.2 %collective-permute-start.11 = (bf16[64,4608]{1,0:T(8,128)(2,1)S(1)}, bf16[64,4608]{1,0:T(8,128)(2,1)}, u32[]{:S(2)}, u32[]{:S(2)}) collective-permute-start(bf16[64,4608]{1,0:T(8,128)(2,1)S(1)} %collective-permute-done.9.refs_2_), channel_id=1, source_target_pairs={{2,0},{4,6},{3,1},{5,7},{10,8},{12,14},{11,9},{13,15},{18,16},{20,... | collective-permute-start | bytes 1769480 | tf_op jit(solution)/shard_map/ppermute | solution.py:30
  108.8 59.9 %collective-permute-start.4 = (bf16[64,4608]{1,0:T(8,128)(2,1)S(1)}, bf16[64,4608]{1,0:T(8,128)(2,1)}, u32[]{:S(2)}, u32[]{:S(2)}) collective-permute-start(bf16[64,4608]{1,0:T(8,128)(2,1)S(1)} %get-tuple-element.47.refs_0_), channel_id=1, source_target_pairs={{0,2},{2,0},{4,6},{6,4},{1,3},{3,1},{5,7},{7,5},{8,10},{10,8},{12,... | collective-permute-start | bytes 1769480 | tf_op jit(solution)/shard_map/ppermute | solution.py:16
  135.4 34.7 %collective-permute-start.6 = (bf16[64,4608]{1,0:T(8,128)(2,1)S(1)}, bf16[64,4608]{1,0:T(8,128)(2,1)}, u32[]{:S(2)}, u32[]{:S(2)}) collective-permute-start(bf16[64,4608]{1,0:T(8,128)(2,1)S(1)} %get-tuple-element.47.refs_0_), channel_id=1, source_target_pairs={{2,4},{4,2},{3,5},{5,3},{10,12},{12,10},{11,13},{13,11},{18,20},{2... | collective-permute-start | bytes 1769480 | tf_op jit(solution)/shard_map/ppermute | solution.py:24
  144.7 36.4 %collective-permute-start.7 = (bf16[64,4608]{1,0:T(8,128)(2,1)S(1)}, bf16[64,4608]{1,0:T(8,128)(2,1)S(1)}, u32[]{:S(2)}, u32[]{:S(2)}) collective-permute-start(bf16[64,4608]{1,0:T(8,128)(2,1)S(1)} %collective-permute-done.5.refs_2_), channel_id=1, source_target_pairs={{2,0},{4,6},{3,1},{5,7},{10,8},{12,14},{11,9},{13,15},{18,16},{20,... | collective-permute-start | bytes 1769480 | tf_op jit(solution)/shard_map/ppermute | solution.py:30
  181.2 29.2 %collective-permute-start.17 = (bf16[64,4608]{1,0:T(8,128)(2,1)}, bf16[64,4608]{1,0:T(8,128)(2,1)S(1)}, u32[]{:S(2)}, u32[]{:S(2)}) collective-permute-start(bf16[64,4608]{1,0:T(8,128)(2,1)} %get-tuple-element.56), channel_id=1, source_target_pairs={{0,16},{8,24},{16,0},{24,8},{1,17},{9,25},{17,1},{25,9},{2,18},{10... | collective-permute-start | bytes 1769480 | tf_op jit(solution)/shard_map/ppermute | solution.py:16
  186.0 36.2 %collective-permute-start.20 = (bf16[64,4608]{1,0:T(8,128)(2,1)}, bf16[64,4608]{1,0:T(8,128)(2,1)}, u32[]{:S(2)}, u32[]{:S(2)}) collective-permute-start(bf16[64,4608]{1,0:T(8,128)(2,1)} %get-tuple-element.59), channel_id=1, source_target_pairs={{0,24},{8,16},{16,8},{24,0},{1,25},{9,17},{17,9},{25,1},{2,26},{10... | collective-permute-start | bytes 1769480 | tf_op jit(solution)/shard_map/ppermute | solution.py:16
  197.6 38.2 %collective-permute-start.16 = (bf16[64,4608]{1,0:T(8,128)(2,1)}, bf16[64,4608]{1,0:T(8,128)(2,1)}, u32[]{:S(2)}, u32[]{:S(2)}) collective-permute-start(bf16[64,4608]{1,0:T(8,128)(2,1)} %get-tuple-element.55), channel_id=1, source_target_pairs={{0,16},{8,24},{16,0},{24,8},{1,17},{9,25},{17,1},{25,9},{2,18},{10... | collective-permute-start | bytes 1769480 | tf_op jit(solution)/shard_map/ppermute | solution.py:16
  210.4 36.0 %collective-permute-start.19 = (bf16[64,4608]{1,0:T(8,128)(2,1)}, bf16[64,4608]{1,0:T(8,128)(2,1)}, u32[]{:S(2)}, u32[]{:S(2)}) collective-permute-start(bf16[64,4608]{1,0:T(8,128)(2,1)} %get-tuple-element.58), channel_id=1, source_target_pairs={{0,24},{8,16},{16,8},{24,0},{1,25},{9,17},{17,9},{25,1},{2,26},{10... | collective-permute-start | bytes 1769480 | tf_op jit(solution)/shard_map/ppermute | solution.py:16
  222.1 49.0 %collective-permute-start.27 = (bf16[32,4608]{1,0:T(8,128)(2,1)S(1)}, bf16[32,4608]{1,0:T(8,128)(2,1)S(1)}, u32[]{:S(2)}, u32[]{:S(2)}) collective-permute-start(bf16[32,4608]{1,0:T(8,128)(2,1)S(1)} %copy-done.9), channel_id=1, source_target_pairs={{2,4},{4,2},{3,5},{5,3},{10,12},{12,10},{11,13},{13,11},{18,20},{2... | collective-permute-start | bytes 884744 | tf_op jit(solution)/shard_map/ppermute | solution.py:24
  222.8 53.4 %collective-permute-start.29 = (bf16[32,4608]{1,0:T(8,128)(2,1)S(1)}, bf16[32,4608]{1,0:T(8,128)(2,1)S(1)}, u32[]{:S(2)}, u32[]{:S(2)}) collective-permute-start(bf16[32,4608]{1,0:T(8,128)(2,1)S(1)} %copy-done.7), channel_id=1, source_target_pairs={{0,2},{2,0},{4,6},{6,4},{1,3},{3,1},{5,7},{7,5},{8,10},{10,8},{12,... | collective-permute-start | bytes 884744 | tf_op jit(solution)/shard_map/ppermute | solution.py:16
  235.8 40.5 %collective-permute-start.31 = (bf16[32,4608]{1,0:T(8,128)(2,1)S(1)}, bf16[32,4608]{1,0:T(8,128)(2,1)S(1)}, u32[]{:S(2)}, u32[]{:S(2)}) collective-permute-start(bf16[32,4608]{1,0:T(8,128)(2,1)S(1)} %copy-done.7), channel_id=1, source_target_pairs={{2,4},{4,2},{3,5},{5,3},{10,12},{12,10},{11,13},{13,11},{18,20},{2... | collective-permute-start | bytes 884744 | tf_op jit(solution)/shard_map/ppermute | solution.py:24
  247.7 28.6 %collective-permute-start.32 = (bf16[32,4608]{1,0:T(8,128)(2,1)}, bf16[32,4608]{1,0:T(8,128)(2,1)S(1)}, u32[]{:S(2)}, u32[]{:S(2)}) collective-permute-start(bf16[32,4608]{1,0:T(8,128)(2,1)} %collective-permute-done.30.refs_2_), channel_id=1, source_target_pairs={{2,0},{4,6},{3,1},{5,7},{10,8},{12,14},{11,9},{13,15},{18,16},{20,... | collective-permute-start | bytes 884744 | tf_op jit(solution)/shard_map/ppermute | solution.py:30
  271.2 49.1 %collective-permute-start.22 = (bf16[2,2,192,576]{3,2,1,0:T(8,128)(2,1)}, bf16[2,2,192,576]{3,2,1,0:T(8,128)(2,1)S(1)}, u32[]{:S(2)}, u32[]{:S(2)}) collective-permute-start(bf16[2,2,192,576]{3,2,1,0:T(8,128)(2,1)} %get-tuple-element.63), channel_id=1, source_target_pairs={{0,8},{8,0},{16,24},{24,16},{1,9},{9,1},{17,25},{25,17},{2,10},{10... | collective-permute-start | bytes 2654216 | tf_op jit(solution)/shard_map/ppermute | solution.py:16
  410.3 29.7 %collective-permute-start.60 = (bf16[768,576]{0,1:T(8,128)(2,1)}, bf16[768,576]{0,1:T(8,128)(2,1)S(1)}, u32[]{:S(2)}, u32[]{:S(2)}) collective-permute-start(bf16[768,576]{0,1:T(8,128)(2,1)} %copy.7), channel_id=1, source_target_pairs={{0,1},{1,0},{2,3},{3,2},{4,5},{5,4},{6,7},{7,6},{8,9},{9,8},{10,11... | collective-permute-start | bytes 2654216 | tf_op jit(solution)/shard_map/ppermute | solution.py:16
  (91 other events, 1881.2 us)

commit v2 on v1

--- a/solution.py
+++ b/solution.py
@@ -8,7 +8,7 @@
 from jax.sharding import Mesh, PartitionSpec as P
 
 
-SHARES = (4, 4, 4, 2, 2)
+SHARES = (5, 4, 3, 2, 2)
 GROUPS = ((0, 1, 2), (3, 4))
 
 
@@ -66,52 +66,137 @@
     )(jnp.stack([by, at_end.astype(jnp.int32)]), *blocks)
 
 
-def product_kernel(toks, subs, chunks, *refs):
-    lefts, weights = refs[: toks * chunks], refs[toks * chunks : toks * chunks + subs]
-    keep, send, total = refs[toks * chunks + subs :]
+def product_kernel(count, *refs):
+    lefts, weight = refs[:count], refs[count]
+    outs, (left, total) = refs[count + 1 : -2], refs[-2:]
     step = pl.program_id(0)
-    left = jnp.concatenate([ref[...] for ref in lefts], axis=0)
-    n = left.shape[0] // toks
-    for k in range(subs):
-        term = contract_last(left, weights[k][...])
-
-        @pl.when(step == 0)
-        def _(k=k, term=term):
-            total[k] = term
-
-        @pl.when(step > 0)
-        def _(k=k, term=term):
-            total[k] += term
+    at = 0
+    for ref in lefts:
+        left[at : at + ref.shape[0]] = ref[...]
+        at += ref.shape[0]
+    term = contract_last(left[...], weight[...])
+
+    @pl.when(step == 0)
+    def _():
+        total[...] = term
+
+    @pl.when(step > 0)
+    def _():
+        total[...] += term
 
     @pl.when(step == pl.num_programs(0) - 1)
     def _():
-        for k in range(subs):
-            for d in range(0, toks, 2):
-                keep[k, d // 2] = total[k, d * n : (d + 1) * n]
-                send[k, d // 2] = total[k, (d + 1) * n : (d + 2) * n].astype(send.dtype)
-
-
-def product(lefts, weights):
-    toks, chunks, subs = len(lefts), len(lefts[0]), len(weights)
+        for d, out in enumerate(outs):
+            n = out.shape[0]
+            out[...] = total[d * n : (d + 1) * n].astype(out.dtype)
+
+
+def product(lefts, weight, dtypes):
+    cols, depth = weight.shape
     n = sum(piece.shape[0] for piece in lefts[0])
-    cols, depth = weights[0].shape
-    tile = depth // 4 if depth % 512 == 0 else depth
+    rows = n * len(lefts)
+    tile = depth // 3 if depth % 768 == 0 and depth > 1536 else depth
     flat = [piece for pieces in lefts for piece in pieces]
-    shape = (subs, toks // 2, n, cols)
-    whole = pl.BlockSpec(shape, lambda i: (0, 0, 0, 0))
-    return pl.pallas_call(
-        functools.partial(product_kernel, toks, subs, chunks),
+    return pl.pallas_call(
+        functools.partial(product_kernel, len(flat)),
         grid=(depth // tile,),
-        in_specs=[pl.BlockSpec((piece.shape[0], tile), lambda i: (0, i)) for piece in flat]
-        + [pl.BlockSpec((cols, tile), lambda i: (0, i))] * subs,
-        out_specs=[whole, whole],
-        out_shape=[jax.ShapeDtypeStruct(shape, jnp.float32), jax.ShapeDtypeStruct(shape, jnp.bfloat16)],
-        scratch_shapes=[pltpu.VMEM((subs, toks * n, cols), jnp.float32)],
-        cost_estimate=pl.CostEstimate(
-            flops=2 * toks * n * cols * depth * subs, bytes_accessed=2 * depth * (toks * n + cols * subs), transcendentals=0
-        ),
+        in_specs=[pl.BlockSpec((piece.shape[0], tile), lambda i: (0, i)) for piece in flat] + [pl.BlockSpec((cols, tile), lambda i: (0, i))],
+        out_specs=[pl.BlockSpec((n, cols), lambda i: (0, 0))] * len(lefts),
+        out_shape=[jax.ShapeDtypeStruct((n, cols), dtype) for dtype in dtypes],
+        scratch_shapes=[pltpu.VMEM((rows, tile), weight.dtype), pltpu.VMEM((rows, cols), jnp.float32)],
+        cost_estimate=pl.CostEstimate(flops=2 * rows * cols * depth, bytes_accessed=2 * depth * (rows + cols), transcendentals=0),
         name="product",
-    )(*flat, *weights)
+    )(*flat, weight)
+
+
+def total_kernel(*refs):
+    total = refs[0][...]
+    for ref in refs[1:-1]:
+        total += ref[...].astype(jnp.float32)
+    refs[-1][...] = total.astype(refs[-1].dtype)
+
+
+def total_of(own, others):
+    return pl.pallas_call(
+        total_kernel,
+        out_shape=jax.ShapeDtypeStruct(own.shape, jnp.bfloat16),
+        cost_estimate=pl.CostEstimate(flops=own.size * len(others), bytes_accessed=2 * own.size * (len(others) + 3), transcendentals=0),
+        name="total",
+    )(own, *others)
+
+
+def hessian_kernel(toks, subs, more, scaling, sub_ref, *refs):
+    out, refs = refs[-1], refs[:-1]
+    before, refs = (refs[0], refs[1:]) if more else (None, refs)
+    left = jnp.concatenate([ref[...] for ref in refs[:toks]], axis=0)
+    cols = left.shape[1]
+    for k in range(subs):
+        right = jnp.concatenate([ref[...] for ref in refs[toks * (k + 1) : toks * (k + 2)]], axis=0)
+        term = contract_rows(left, right) * scaling
+        for by in range(subs):
+
+            @pl.when(sub_ref[0] == by)
+            def _(k=k, by=by, term=term):
+                at = slice((by ^ k) * cols, ((by ^ k) + 1) * cols)
+                out[:, at] = term + before[:, at] if more else term
+
+
+def hessian_of(left, right, scaling, before, sub):
+    toks, subs = len(left), len(right)
+    n, cols = left[0].shape
+    flat = list(left) + [piece for pieces in right for piece in pieces]
+    extra = [] if before is None else [before]
+    return pl.pallas_call(
+        functools.partial(hessian_kernel, toks, subs, len(extra), scaling),
+        in_specs=[pl.BlockSpec(memory_space=pltpu.SMEM)] + [pl.BlockSpec(memory_space=pltpu.VMEM)] * (len(flat) + len(extra)),
+        out_specs=pl.BlockSpec(memory_space=pltpu.VMEM),
+        out_shape=jax.ShapeDtypeStruct((cols, subs * cols), jnp.float32),
+        cost_estimate=pl.CostEstimate(flops=2 * toks * n * cols * cols * subs, bytes_accessed=4 * cols * cols * subs, transcendentals=0),
+        name="hessian",
+    )(sub.reshape(1), *extra, *flat)
+
+
+def pick_kernel(toks, subs, share, at_ref, *refs):
+    outs, sems = refs[-subs - 1 : -1], refs[-1]
+    groups, at = [], 0
+    count = (len(refs) - subs - 1) // len(GROUPS)
+    for g in range(len(GROUPS)):
+        blocks = refs[g * count : (g + 1) * count]
+        groups.append((at, blocks))
+        at += blocks[0].shape[0]
+    row, sub, at_end = at_ref[0], at_ref[1], at_ref[2]
+    for k in range(subs):
+        first = (row * subs + (sub ^ k)) * share
+        for q in range(toks):
+            b = q ^ row
+            b = jnp.where((b == toks - 1) & (at_end == 1), count - 1, b)
+            for start, blocks in groups:
+                for i, block in enumerate(blocks):
+
+                    @pl.when((b == i) & (first >= start) & (first < start + block.shape[0]))
+                    def _(k=k, q=q, block=block, first=first, start=start):
+                        rows = block.at[pl.ds(pl.multiple_of(first - start, share), share)]
+                        pltpu.make_async_copy(rows, outs[k].at[q], sems.at[k, q]).start()
+
+    for k in range(subs):
+        for q in range(toks):
+            pltpu.make_async_copy(refs[0].at[pl.ds(0, share)], outs[k].at[q], sems.at[k, q]).wait()
+
+
+def pick(layer_rows, share, subs):
+    toks, row = lax.axis_size("row"), lax.axis_index("row")
+    cols = layer_rows[0][0].shape[1]
+    flat = [block for blocks in layer_rows for block in blocks]
+    at_end = ((row == 0) | (row == toks - 1)).astype(jnp.int32)
+    return pl.pallas_call(
+        functools.partial(pick_kernel, toks, subs, share),
+        in_specs=[pl.BlockSpec(memory_space=pltpu.SMEM)] + [pl.BlockSpec(memory_space=pltpu.HBM)] * len(flat),
+        out_specs=[pl.BlockSpec(memory_space=pltpu.VMEM)] * subs,
+        out_shape=[jax.ShapeDtypeStruct((toks, share, cols), flat[0].dtype)] * subs,
+        scratch_shapes=[pltpu.SemaphoreType.DMA((subs, toks))],
+        cost_estimate=pl.CostEstimate(flops=0, bytes_accessed=4 * subs * toks * share * cols, transcendentals=0),
+        name="pick",
+    )(jnp.stack([row, lax.axis_index("sub"), at_end]), *flat)
 
 
 def select_order(blocks, by):
@@ -161,40 +246,28 @@
         blocks = spread_last(seen[j], "row")
         arrived.append(turn(xor_order(blocks, tok ^ row, "row"), "tok"))
 
-    left, right, layer_rows = [], [], []
+    def across(value, d, k):
+        pairs = [(t * subs + s, (t ^ d) * subs + (s ^ k)) for t in range(toks) for s in range(subs)]
+        return lax.ppermute(value, ("tok", "sub"), pairs) if d or k else value
+
+    hessian, layer_rows = None, []
+    scaling = 2.0 / (rows * toks)
     for group in GROUPS:
-        keep, send = product([[arrived[j][d] for j in group] for d in range(toks)], weights)
-        total = keep + swap(send, "tok", 1).astype(jnp.float32)
-        rest = total[1:].astype(small)
-        total = total[0]
-        for k in range(1, subs):
-            total = total + swap(rest[k - 1], "sub", k).astype(jnp.float32)
-        bit = 2
-        while bit < toks:
-            total = total.reshape((-1, 2) + total.shape[1:])
-            total = total[:, 0] + swap(total[:, 1].astype(small), "tok", bit).astype(jnp.float32)
-            bit *= 2
-        layer = total[0].astype(small)
+        lefts = [[arrived[j][d] for j in group] for d in range(toks)]
+        terms = [product(lefts, weights[k], [small if k or d else jnp.float32 for d in range(toks)]) for k in range(subs)]
+        others = [across(terms[k][d], d, k) for k in reversed(range(subs)) for d in range(toks) if d or k]
+        layer = total_of(terms[0][0], others)
         blocks = spread(layer, "row")
-        left.append(jnp.concatenate(turn([layer] * toks, "tok"), axis=0))
         layer_rows.append(blocks)
-        mine = jnp.concatenate(turn(xor_order(blocks, tok ^ row, "row"), "tok"), axis=0)
-        both = [mine] + [swap(mine, "sub", k) for k in range(1, subs)]
-        right.append(jnp.concatenate(select_order(both, sub), axis=1))
-
-    scaling = 2.0 / (rows * toks)
-    hessian = contract_rows(jnp.concatenate(left, axis=0), jnp.concatenate(right, axis=0)) * scaling
+        mine = xor_order(blocks, tok ^ row, "row")
+        left = turn([layer] * toks, "tok")
+        right = [[across(mine[d], d, k) for d in range(toks)] for k in range(subs)]
+        hessian = hessian_of(left, right, scaling, hessian, sub)
 
     share = rows // (toks * subs)
-    whole = [jnp.concatenate(blocks, axis=0) for blocks in zip(*layer_rows)]
-    whole = jnp.stack(xor_order(whole, row, "row"), axis=0).reshape(toks, toks, subs, share, cols)
-
-    def for_sub(other):
-        return lax.dynamic_slice(whole, (0, row, other, 0, 0), (toks, 1, 1, share, cols)).reshape(toks * share, cols)
-
-    pieces = [for_sub(sub)] + [swap(for_sub(sub ^ k), "sub", k) for k in range(1, subs)]
-    pieces = [piece.reshape(toks, share, cols) for piece in select_order(pieces, sub)]
-    layer_out = jnp.stack(pieces, axis=1).transpose(2, 0, 1, 3).reshape(share, toks * subs * cols)
+    pieces = pick(layer_rows, share, subs)
+    pieces = list(pieces[:1]) + [swap(pieces[k], "sub", k) for k in range(1, subs)]
+    layer_out = jnp.stack(select_order(pieces, sub), axis=1).transpose(2, 0, 1, 3).reshape(share, toks * subs * cols)
     return layer_out, hessian
 
 

time: 446 us -> 459 us (1.029)
  Pallas kernels: 55.8 us -> 71.9 us
  starting transfers between devices: 94.4 us -> 102 us
  other arithmetic: 28.4 us -> 21.4 us
  local copies, waits for them, and re-layouts: 11.6 us -> 5.8 us
    ppermute x51 -> x37, waiting for transfers between devices: 222 us -> 193 us  [swap(): lax.ppermute(value, axis, [(i, i ^ offset) for i in range(lax.axis_size(a...]
    ppermute x0 -> x28, waiting for transfers between devices: none -> 28.6 us  [across(): return lax.ppermute(value, ('tok', 'sub'), pairs) if d or k else value]
    ppermute x0 -> x28, starting transfers between devices: none -> 28 us  [across(): return lax.ppermute(value, ('tok', 'sub'), pairs) if d or k else value]
    pallas_call x2 -> x9, Pallas kernels: 32.6 us -> 51.6 us  [the longest x4 32.8 us: product(): pl.pallas_call(functools.partial(product_kernel, len(flat)), grid=(depth...]
    ppermute x51 -> x37, starting transfers between devices: 79.4 us -> 60.4 us  [swap(): lax.ppermute(value, axis, [(i, i ^ offset) for i in range(lax.axis_size(a...]
    concatenate x5 -> x0, other arithmetic: 4.79 us -> none  [body(): whole = [jnp.concatenate(blocks, axis=0) for blocks in zip(*layer_rows)]]
    pallas_call x8 -> x7, Pallas kernels: 23.2 us -> 20.3 us  [xor_order(): pl.pallas_call(functools.partial(order_kernel, size), in_specs=[pl.BlockS...]
  transfers between devices with their start and end apart: 65 -> 79, of which waited for: 27 -> 29; matrix products, arithmetic and copies ran while one was open for 5% -> 3% of each run, Pallas kernels for 13% -> 15%
where the time goes in v2:
time: 459 us; the launch traced here: 458 us
  waiting for transfers between devices  255 us (56%)
  starting transfers between devices  102 us (22%)
  Pallas kernels  71.9 us (16%)
  other arithmetic  21.4 us (5%)
  local copies, waits for them, and re-layouts  5.8 us (1%)
    ppermute x37, waiting for transfers between devices, swap(): lax.ppermute(value, axis, [(i, i ^ offset) for i in range(lax.axis_size(a...  193 us
    ppermute x37, starting transfers between devices, swap(): lax.ppermute(value, axis, [(i, i ^ offset) for i in range(lax.axis_size(a...  60.4 us
    ppermute x7, waiting for transfers between devices, spread_last(): return list(blocks) + [lax.ppermute(blocks[2], axis, [(1, 0), (2, 3)])]  33.1 us
    pallas_call x4, Pallas kernels, product(): pl.pallas_call(functools.partial(product_kernel, len(flat)), grid=(depth...  32.8 us
    ppermute x28, waiting for transfers between devices, across(): return lax.ppermute(value, ('tok', 'sub'), pairs) if d or k else value  28.6 us
    ppermute x28, starting transfers between devices, across(): return lax.ppermute(value, ('tok', 'sub'), pairs) if d or k else value  28 us
    pallas_call x7, Pallas kernels, xor_order(): pl.pallas_call(functools.partial(order_kernel, size), in_specs=[pl.BlockS...  20.3 us
    mul x2, other arithmetic, pruned(): w * lax.dynamic_slice(mask, (0, block * depth), (cols, depth)).astype(w.d...  19.3 us
  transfers between devices with their start and end apart: 79, of which 29 were waited for; matrix products, arithmetic and copies ran while one was open for 3% of the time, Pallas kernels for 15%

profile of v2, /device:TPU:0, one launch (start us, length us, event | category | flops | bytes accessed | tf_op | source)
XLA Modules:
  0.0 457.7 jit_solution(17126415620435394255)
XLA Ops:
  0.7 9.7 %fusion.1 = bf16[576,4608]{1,0:T(8,128)(2,1)} fusion(s32[576,9216]{1,0:T(8,128)} %param.5, s32[]{:T(128)S(6)} %select_n.15, bf16[576,9216]{1,0:T(8,128)(2,1)} %param.4), kind=kLoop, calls=%fused_computation.3 | loop fusion | flops 13271040 | bytes 21233668 | tf_op jit(solution)/shard_map/mul | solution.py:235
  19.5 14.6 %collective-permute-start.9 = (bf16[48,4608]{1,0:T(8,128)(2,1)S(1)}, bf16[48,4608]{1,0:T(8,128)(2,1)S(1)}, u32[]{:S(2)}, u32[]{:S(2)}) collective-permute-start(bf16[48,4608]{1,0:T(8,128)(2,1)S(1)} %slice.17.refs_0_), channel_id=1, source_target_pairs={{0,4},{2,6},{4,0},{6,2},{1,5},{3,7},{5,1},{7,3},{8,12},{10,14},{12... | collective-permute-start | bytes 1327112 | tf_op jit(solution)/shard_map/ppermute | solution.py:16
  34.1 14.4 %collective-permute-done.34.refs_2_ = bf16[32,4608]{1,0:T(8,128)(2,1)S(1)} collective-permute-done((bf16[32,4608]{1,0:T(8,128)(2,1)S(1)}, bf16[32,4608]{1,0:T(8,128)(2,1)S(1)}, u32[]{:S(2)}, u32[]{:S(2)}) %collective-permute-start.34) | collective-permute-done | bytes 294944 | tf_op jit(solution)/shard_map/ppermute | solution.py:16
  48.5 6.1 %collective-permute-start.8 = (bf16[48,4608]{1,0:T(8,128)(2,1)S(1)}, bf16[48,4608]{1,0:T(8,128)(2,1)S(1)}, u32[]{:S(2)}, u32[]{:S(2)}) collective-permute-start(bf16[48,4608]{1,0:T(8,128)(2,1)S(1)} %slice.17.refs_0_), channel_id=1, source_target_pairs={{0,2},{2,0},{4,6},{6,4},{1,3},{3,1},{5,7},{7,5},{8,10},{10,8},{12,... | collective-permute-start | bytes 1327112 | tf_op jit(solution)/shard_map/ppermute | solution.py:16
  54.7 24.1 %collective-permute-done.38.refs_2_ = bf16[32,4608]{1,0:T(8,128)(2,1)} collective-permute-done((bf16[32,4608]{1,0:T(8,128)(2,1)S(1)}, bf16[32,4608]{1,0:T(8,128)(2,1)}, u32[]{:S(2)}, u32[]{:S(2)}) %collective-permute-start.38) | collective-permute-done | bytes 294944 | tf_op jit(solution)/shard_map/ppermute | solution.py:16
  91.1 46.1 %collective-permute-done.5.refs_2_ = bf16[64,4608]{1,0:T(8,128)(2,1)} collective-permute-done((bf16[64,4608]{1,0:T(8,128)(2,1)S(1)}, bf16[64,4608]{1,0:T(8,128)(2,1)}, u32[]{:S(2)}, u32[]{:S(2)}) %collective-permute-start.5) | collective-permute-done | bytes 589856 | tf_op jit(solution)/shard_map/ppermute | solution.py:16
  139.2 13.6 %collective-permute-done.1.refs_2_ = bf16[80,4608]{1,0:T(8,128)(2,1)S(1)} collective-permute-done((bf16[80,4608]{1,0:T(8,128)(2,1)S(1)}, bf16[80,4608]{1,0:T(8,128)(2,1)S(1)}, u32[]{:S(2)}, u32[]{:S(2)}) %collective-permute-start.1) | collective-permute-done | bytes 737312 | tf_op jit(solution)/shard_map/ppermute | solution.py:16
  152.8 7.4 %collective-permute-done.11.refs_4_ = bf16[48,4608]{1,0:T(8,128)(2,1)S(1)} collective-permute-done((bf16[48,4608]{1,0:T(8,128)(2,1)S(1)}, bf16[48,4608]{1,0:T(8,128)(2,1)S(1)}, u32[]{:S(2)}, u32[]{:S(2)}) %collective-permute-start.11) | collective-permute-done | bytes 442400 | tf_op jit(solution)/shard_map/ppermute | solution.py:30
  165.9 7.1 %collective-permute-done.7.refs_4_ = bf16[64,4608]{1,0:T(8,128)(2,1)} collective-permute-done((bf16[64,4608]{1,0:T(8,128)(2,1)}, bf16[64,4608]{1,0:T(8,128)(2,1)}, u32[]{:S(2)}, u32[]{:S(2)}) %collective-permute-start.7) | collective-permute-done | bytes 589856 | tf_op jit(solution)/shard_map/ppermute | solution.py:30
  176.8 11.9 %collective-permute-done.refs_1_ = bf16[80,4608]{1,0:T(8,128)(2,1)S(1)} collective-permute-done((bf16[80,4608]{1,0:T(8,128)(2,1)S(1)}, bf16[80,4608]{1,0:T(8,128)(2,1)S(1)}, u32[]{:S(2)}, u32[]{:S(2)}) %collective-permute-start) | collective-permute-done | bytes 737312 | tf_op jit(solution)/shard_map/ppermute | solution.py:16
  190.7 13.1 %collective-permute-done.3.refs_4_ = bf16[80,4608]{1,0:T(8,128)(2,1)} collective-permute-done((bf16[80,4608]{1,0:T(8,128)(2,1)S(1)}, bf16[80,4608]{1,0:T(8,128)(2,1)}, u32[]{:S(2)}, u32[]{:S(2)}) %collective-permute-start.3) | collective-permute-done | bytes 737312 | tf_op jit(solution)/shard_map/ppermute | solution.py:30
  207.7 6.9 %collective-permute-done.17.refs_8_ = bf16[48,4608]{1,0:T(8,128)(2,1)} collective-permute-done((bf16[48,4608]{1,0:T(8,128)(2,1)}, bf16[48,4608]{1,0:T(8,128)(2,1)}, u32[]{:S(2)}, u32[]{:S(2)}) %collective-permute-start.17) | collective-permute-done | bytes 442400 | tf_op jit(solution)/shard_map/ppermute | solution.py:16
  214.7 6.1 %collective-permute-done.20.refs_11_ = bf16[48,4608]{1,0:T(8,128)(2,1)} collective-permute-done((bf16[48,4608]{1,0:T(8,128)(2,1)}, bf16[48,4608]{1,0:T(8,128)(2,1)}, u32[]{:S(2)}, u32[]{:S(2)}) %collective-permute-start.20) | collective-permute-done | bytes 442400 | tf_op jit(solution)/shard_map/ppermute | solution.py:16
  225.9 9.6 %fusion.refs_12_.refs_8_ = bf16[576,4608]{1,0:T(8,128)(2,1)} fusion(s32[576,9216]{1,0:T(8,128)} %param.5, s32[]{:T(128)S(6)} %select_n.14, bf16[576,9216]{1,0:T(8,128)(2,1)} %param.4), kind=kLoop, calls=%fused_computation.2 | loop fusion | flops 13271040 | bytes 21233668 | tf_op jit(solution)/shard_map/mul | solution.py:235
  235.5 33.1 %collective-permute-done.19.refs_10_ = bf16[64,4608]{1,0:T(8,128)(2,1)} collective-permute-done((bf16[64,4608]{1,0:T(8,128)(2,1)}, bf16[64,4608]{1,0:T(8,128)(2,1)}, u32[]{:S(2)}, u32[]{:S(2)}) %collective-permute-start.19) | collective-permute-done | bytes 589856 | tf_op jit(solution)/shard_map/ppermute | solution.py:16
  271.7 10.2 %product.4 = (f32[192,576]{1,0:T(8,128)}, bf16[192,576]{1,0:T(8,128)(2,1)}, bf16[192,576]{1,0:T(8,128)(2,1)}, bf16[192,576]{1,0:T(8,128)(2,1)}) custom-call(bf16[80,4608]{1,0:T(8,128)(2,1)} %get-tuple-element.56.refs_0_, bf16[64,4608]{1,0:T(8,128)(2,1)} %get-tuple-element.58.refs_1_, bf16[48,4608]{1,0:T(8,128)(2,1)} %get-tuple-element.60.refs_2_, ...), custom_call_target="tpu_custom_call" | custom-call | flops 4076863488 | bytes 12386304 | tf_op jit(solution)/shard_map/product/pallas_call | solution.py:100
  283.4 10.2 %product.5 = (bf16[192,576]{1,0:T(8,128)(2,1)}, bf16[192,576]{1,0:T(8,128)(2,1)}, bf16[192,576]{1,0:T(8,128)(2,1)}, bf16[192,576]{1,0:T(8,128)(2,1)}) custom-call(bf16[80,4608]{1,0:T(8,128)(2,1)} %get-tuple-element.56.refs_0_, bf16[64,4608]{1,0:T(8,128)(2,1)} %get-tuple-element.58.refs_1_, bf16[48,4608]{1,0:T(8,128)(2,1)} %get-tuple-element.60.refs_2_, ...), custom_call_target="tpu_custom_call" | custom-call | flops 4076863488 | bytes 12386304 | tf_op jit(solution)/shard_map/product/pallas_call | solution.py:100
  303.1 10.7 %collective-permute-done.22.refs_1_ = bf16[192,576]{1,0:T(8,128)(2,1)S(1)} collective-permute-done((bf16[192,576]{1,0:T(8,128)(2,1)}, bf16[192,576]{1,0:T(8,128)(2,1)S(1)}, u32[]{:S(2)}, u32[]{:S(2)}) %collective-permute-start.22) | collective-permute-done | bytes 221216 | tf_op jit(solution)/shard_map/ppermute | solution.py:251
  331.4 6.3 %collective-permute-done.46.refs_7_ = bf16[32,4608]{1,0:T(8,128)(2,1)S(1)} collective-permute-done((bf16[32,4608]{1,0:T(8,128)(2,1)}, bf16[32,4608]{1,0:T(8,128)(2,1)S(1)}, u32[]{:S(2)}, u32[]{:S(2)}) %collective-permute-start.46) | collective-permute-done | bytes 294944 | tf_op jit(solution)/shard_map/ppermute | solution.py:16
  338.5 6.2 %product.6 = (f32[64,576]{1,0:T(8,128)}, bf16[64,576]{1,0:T(8,128)(2,1)}, bf16[64,576]{1,0:T(8,128)(2,1)}, bf16[64,576]{1,0:T(8,128)(2,1)}) custom-call(bf16[32,4608]{1,0:T(8,128)(2,1)} %get-tuple-element.81.refs_0_, bf16[32,4608]{1,0:T(8,128)(2,1)} %get-tuple-element.83.refs_1_, bf16[32,4608]{1,0:T(8,128)(2,1)} %copy-done.9, bf16[32,4608]{1,0:T(8,128)(2,1)} %copy-done.12, ...), custom_call_target="tpu_custom_call" | custom-call | flops 1358954496 | bytes 7667712 | tf_op jit(solution)/shard_map/product/pallas_call | solution.py:100
  346.6 6.2 %product.7 = (bf16[64,576]{1,0:T(8,128)(2,1)}, bf16[64,576]{1,0:T(8,128)(2,1)}, bf16[64,576]{1,0:T(8,128)(2,1)}, bf16[64,576]{1,0:T(8,128)(2,1)}) custom-call(bf16[32,4608]{1,0:T(8,128)(2,1)} %get-tuple-element.81.refs_0_, bf16[32,4608]{1,0:T(8,128)(2,1)} %get-tuple-element.83.refs_1_, bf16[32,4608]{1,0:T(8,128)(2,1)} %copy-done.9, ...), custom_call_target="tpu_custom_call" | custom-call | flops 1358954496 | bytes 7667712 | tf_op jit(solution)/shard_map/product/pallas_call | solution.py:100
  366.5 7.2 %collective-permute-start.29 = (bf16[192,576]{1,0:T(8,128)(2,1)S(1)}, bf16[192,576]{1,0:T(8,128)(2,1)S(1)}, u32[]{:S(2)}, u32[]{:S(2)}) collective-permute-start(bf16[192,576]{1,0:T(8,128)(2,1)S(1)} %copy-done), channel_id=1, source_target_pairs={{0,2},{2,0},{4,6},{6,4},{1,3},{3,1},{5,7},{7,5},{8,10},{10,8},{12,... | collective-permute-start | bytes 663560 | tf_op jit(solution)/shard_map/ppermute | solution.py:16
  410.2 14.1 %collective-permute-done.58 = bf16[4,32,576]{2,1,0:T(8,128)(2,1)S(1)} collective-permute-done((bf16[4,32,576]{2,1,0:T(8,128)(2,1)}, bf16[4,32,576]{2,1,0:T(8,128)(2,1)S(1)}, u32[]{:S(2)}, u32[]{:S(2)}) %collective-permute-start.58) | collective-permute-done | bytes 147488 | tf_op jit(solution)/shard_map/ppermute | solution.py:16
  444.5 6.4 %hessian.2.refs_0_ = f32[576,1152]{1,0:T(8,128)} custom-call(s32[1]{0:T(128)} %bitcast.1.sub_ref, bf16[192,576]{1,0:T(8,128)(2,1)} %total.2.refs_0_, bf16[192,576]{1,0:T(8,128)(2,1)} %copy-done.41, bf16[192,576]{1,0:T(8,128)(2,1)} %copy-done.40, bf16[192,576]{1,0:T(8,128)(2,1)} %copy-done.39, bf16[192,576]{1,0:T(8,128)(2,1)} %get-tuple-element.100.refs_4_, ...), custom_call_target="tpu_custom_call" | custom-call | flops 1019215872 | bytes 2654208 | tf_op jit(solution)/shard_map/hessian/pallas_call | solution.py:149
  (316 shorter events, 154.6 us)
Async XLA Ops:
  10.4 272.2 %collective-permute-start.21 = (bf16[576,4608]{1,0:T(8,128)(2,1)}, bf16[576,4608]{1,0:T(8,128)(2,1)}, u32[]{:S(2)}, u32[]{:S(2)}) collective-permute-start(bf16[576,4608]{1,0:T(8,128)(2,1)} %fusion.1), channel_id=1, source_target_pairs={{0,1},{1,0},{2,3},{3,2},{4,5},{5,4},{6,7},{7,6},{8,9},{9,8},{10,11... | collective-permute-start | bytes 15925256 | tf_op jit(solution)/shard_map/ppermute | solution.py:16
  14.3 34.2 %collective-permute-start.34 = (bf16[32,4608]{1,0:T(8,128)(2,1)S(1)}, bf16[32,4608]{1,0:T(8,128)(2,1)S(1)}, u32[]{:S(2)}, u32[]{:S(2)}) collective-permute-start(bf16[32,4608]{1,0:T(8,128)(2,1)S(1)} %get-tuple-element.80.refs_0_), channel_id=1, source_target_pairs={{0,4},{2,6},{4,0},{6,2},{1,5},{3,7},{5,1},{7,3},{8,12},{10,14},{12... | collective-permute-start | bytes 884744 | tf_op jit(solution)/shard_map/ppermute | solution.py:16
  18.6 29.9 %collective-permute-start.33 = (bf16[32,4608]{1,0:T(8,128)(2,1)S(1)}, bf16[32,4608]{1,0:T(8,128)(2,1)S(1)}, u32[]{:S(2)}, u32[]{:S(2)}) collective-permute-start(bf16[32,4608]{1,0:T(8,128)(2,1)S(1)} %get-tuple-element.80.refs_0_), channel_id=1, source_target_pairs={{0,2},{2,0},{4,6},{6,4},{1,3},{3,1},{5,7},{7,5},{8,10},{10,8},{12,... | collective-permute-start | bytes 884744 | tf_op jit(solution)/shard_map/ppermute | solution.py:16
  18.8 60.7 %collective-permute-start.10 = (bf16[48,4608]{1,0:T(8,128)(2,1)S(1)}, bf16[48,4608]{1,0:T(8,128)(2,1)S(1)}, u32[]{:S(2)}, u32[]{:S(2)}) collective-permute-start(bf16[48,4608]{1,0:T(8,128)(2,1)S(1)} %slice.17.refs_0_), channel_id=1, source_target_pairs={{2,4},{4,2},{3,5},{5,3},{10,12},{12,10},{11,13},{13,11},{18,20},{2... | collective-permute-start | bytes 1327112 | tf_op jit(solution)/shard_map/ppermute | solution.py:24
  19.5 61.3 %collective-permute-start.9 = (bf16[48,4608]{1,0:T(8,128)(2,1)S(1)}, bf16[48,4608]{1,0:T(8,128)(2,1)S(1)}, u32[]{:S(2)}, u32[]{:S(2)}) collective-permute-start(bf16[48,4608]{1,0:T(8,128)(2,1)S(1)} %slice.17.refs_0_), channel_id=1, source_target_pairs={{0,4},{2,6},{4,0},{6,2},{1,5},{3,7},{5,1},{7,3},{8,12},{10,14},{12... | collective-permute-start | bytes 1327112 | tf_op jit(solution)/shard_map/ppermute | solution.py:16
  48.5 30.3 %collective-permute-start.38 = (bf16[32,4608]{1,0:T(8,128)(2,1)S(1)}, bf16[32,4608]{1,0:T(8,128)(2,1)}, u32[]{:S(2)}, u32[]{:S(2)}) collective-permute-start(bf16[32,4608]{1,0:T(8,128)(2,1)S(1)} %get-tuple-element.82.refs_0_), channel_id=1, source_target_pairs={{0,4},{2,6},{4,0},{6,2},{1,5},{3,7},{5,1},{7,3},{8,12},{10,14},{12... | collective-permute-start | bytes 884744 | tf_op jit(solution)/shard_map/ppermute | solution.py:16
  48.5 36.0 %collective-permute-start.8 = (bf16[48,4608]{1,0:T(8,128)(2,1)S(1)}, bf16[48,4608]{1,0:T(8,128)(2,1)S(1)}, u32[]{:S(2)}, u32[]{:S(2)}) collective-permute-start(bf16[48,4608]{1,0:T(8,128)(2,1)S(1)} %slice.17.refs_0_), channel_id=1, source_target_pairs={{0,2},{2,0},{4,6},{6,4},{1,3},{3,1},{5,7},{7,5},{8,10},{10,8},{12,... | collective-permute-start | bytes 1327112 | tf_op jit(solution)/shard_map/ppermute | solution.py:16
  80.8 56.3 %collective-permute-start.5 = (bf16[64,4608]{1,0:T(8,128)(2,1)S(1)}, bf16[64,4608]{1,0:T(8,128)(2,1)}, u32[]{:S(2)}, u32[]{:S(2)}) collective-permute-start(bf16[64,4608]{1,0:T(8,128)(2,1)S(1)} %slice.16.refs_0_), channel_id=1, source_target_pairs={{0,4},{2,6},{4,0},{6,2},{1,5},{3,7},{5,1},{7,3},{8,12},{10,14},{12... | collective-permute-start | bytes 1769480 | tf_op jit(solution)/shard_map/ppermute | solution.py:16
  84.6 68.2 %collective-permute-start.1 = (bf16[80,4608]{1,0:T(8,128)(2,1)S(1)}, bf16[80,4608]{1,0:T(8,128)(2,1)S(1)}, u32[]{:S(2)}, u32[]{:S(2)}) collective-permute-start(bf16[80,4608]{1,0:T(8,128)(2,1)S(1)} %slice.15.refs_0_), channel_id=1, source_target_pairs={{0,4},{2,6},{4,0},{6,2},{1,5},{3,7},{5,1},{7,3},{8,12},{10,14},{12... | collective-permute-start | bytes 2211848 | tf_op jit(solution)/shard_map/ppermute | solution.py:16
  89.0 49.4 %collective-permute-start.4 = (bf16[64,4608]{1,0:T(8,128)(2,1)S(1)}, bf16[64,4608]{1,0:T(8,128)(2,1)S(1)}, u32[]{:S(2)}, u32[]{:S(2)}) collective-permute-start(bf16[64,4608]{1,0:T(8,128)(2,1)S(1)} %slice.16.refs_0_), channel_id=1, source_target_pairs={{0,2},{2,0},{4,6},{6,4},{1,3},{3,1},{5,7},{7,5},{8,10},{10,8},{12,... | collective-permute-start | bytes 1769480 | tf_op jit(solution)/shard_map/ppermute | solution.py:16
  89.8 70.5 %collective-permute-start.11 = (bf16[48,4608]{1,0:T(8,128)(2,1)S(1)}, bf16[48,4608]{1,0:T(8,128)(2,1)S(1)}, u32[]{:S(2)}, u32[]{:S(2)}) collective-permute-start(bf16[48,4608]{1,0:T(8,128)(2,1)S(1)} %collective-permute-done.9.refs_2_), channel_id=1, source_target_pairs={{2,0},{4,6},{3,1},{5,7},{10,8},{12,14},{11,9},{13,15},{18,16},{20,... | collective-permute-start | bytes 1327112 | tf_op jit(solution)/shard_map/ppermute | solution.py:30
  137.2 35.8 %collective-permute-start.7 = (bf16[64,4608]{1,0:T(8,128)(2,1)}, bf16[64,4608]{1,0:T(8,128)(2,1)}, u32[]{:S(2)}, u32[]{:S(2)}) collective-permute-start(bf16[64,4608]{1,0:T(8,128)(2,1)} %collective-permute-done.5.refs_2_), channel_id=1, source_target_pairs={{2,0},{4,6},{3,1},{5,7},{10,8},{12,14},{11,9},{13,15},{18,16},{20,... | collective-permute-start | bytes 1769480 | tf_op jit(solution)/shard_map/ppermute | solution.py:30
  138.5 37.7 %collective-permute-start.2 = (bf16[80,4608]{1,0:T(8,128)(2,1)S(1)}, bf16[80,4608]{1,0:T(8,128)(2,1)S(1)}, u32[]{:S(2)}, u32[]{:S(2)}) collective-permute-start(bf16[80,4608]{1,0:T(8,128)(2,1)S(1)} %slice.15.refs_0_), channel_id=1, source_target_pairs={{2,4},{4,2},{3,5},{5,3},{10,12},{12,10},{11,13},{13,11},{18,20},{2... | collective-permute-start | bytes 2211848 | tf_op jit(solution)/shard_map/ppermute | solution.py:24
  152.8 35.9 %collective-permute-start = (bf16[80,4608]{1,0:T(8,128)(2,1)S(1)}, bf16[80,4608]{1,0:T(8,128)(2,1)S(1)}, u32[]{:S(2)}, u32[]{:S(2)}) collective-permute-start(bf16[80,4608]{1,0:T(8,128)(2,1)S(1)} %slice.15.refs_0_), channel_id=1, source_target_pairs={{0,2},{2,0},{4,6},{6,4},{1,3},{3,1},{5,7},{7,5},{8,10},{10,8},{12,... | collective-permute-start | bytes 2211848 | tf_op jit(solution)/shard_map/ppermute | solution.py:16
  161.0 42.8 %collective-permute-start.3 = (bf16[80,4608]{1,0:T(8,128)(2,1)S(1)}, bf16[80,4608]{1,0:T(8,128)(2,1)}, u32[]{:S(2)}, u32[]{:S(2)}) collective-permute-start(bf16[80,4608]{1,0:T(8,128)(2,1)S(1)} %collective-permute-done.1.refs_2_), channel_id=1, source_target_pairs={{2,0},{4,6},{3,1},{5,7},{10,8},{12,14},{11,9},{13,15},{18,16},{20,... | collective-permute-start | bytes 2211848 | tf_op jit(solution)/shard_map/ppermute | solution.py:30
  176.2 45.1 %collective-permute-start.13 = (bf16[64,4608]{1,0:T(8,128)(2,1)}, bf16[64,4608]{1,0:T(8,128)(2,1)}, u32[]{:S(2)}, u32[]{:S(2)}) collective-permute-start(bf16[64,4608]{1,0:T(8,128)(2,1)} %get-tuple-element.62), channel_id=1, source_target_pairs={{0,8},{8,0},{16,24},{24,16},{1,9},{9,1},{17,25},{25,17},{2,10},{10... | collective-permute-start | bytes 1769480 | tf_op jit(solution)/shard_map/ppermute | solution.py:16
  188.7 37.1 %collective-permute-start.16 = (bf16[64,4608]{1,0:T(8,128)(2,1)}, bf16[64,4608]{1,0:T(8,128)(2,1)}, u32[]{:S(2)}, u32[]{:S(2)}) collective-permute-start(bf16[64,4608]{1,0:T(8,128)(2,1)} %get-tuple-element.65), channel_id=1, source_target_pairs={{0,16},{8,24},{16,0},{24,8},{1,17},{9,25},{17,1},{25,9},{2,18},{10... | collective-permute-start | bytes 1769480 | tf_op jit(solution)/shard_map/ppermute | solution.py:16
  214.7 54.6 %collective-permute-start.12 = (bf16[80,4608]{1,0:T(8,128)(2,1)}, bf16[80,4608]{1,0:T(8,128)(2,1)S(1)}, u32[]{:S(2)}, u32[]{:S(2)}) collective-permute-start(bf16[80,4608]{1,0:T(8,128)(2,1)} %get-tuple-element.61), channel_id=1, source_target_pairs={{0,8},{8,0},{16,24},{24,16},{1,9},{9,1},{17,25},{25,17},{2,10},{10... | collective-permute-start | bytes 2211848 | tf_op jit(solution)/shard_map/ppermute | solution.py:16
  220.8 49.4 %collective-permute-start.15 = (bf16[80,4608]{1,0:T(8,128)(2,1)}, bf16[80,4608]{1,0:T(8,128)(2,1)S(1)}, u32[]{:S(2)}, u32[]{:S(2)}) collective-permute-start(bf16[80,4608]{1,0:T(8,128)(2,1)} %get-tuple-element.64), channel_id=1, source_target_pairs={{0,16},{8,24},{16,0},{24,8},{1,17},{9,25},{17,1},{25,9},{2,18},{10... | collective-permute-start | bytes 2211848 | tf_op jit(solution)/shard_map/ppermute | solution.py:16
  221.3 50.3 %collective-permute-start.18 = (bf16[80,4608]{1,0:T(8,128)(2,1)}, bf16[80,4608]{1,0:T(8,128)(2,1)}, u32[]{:S(2)}, u32[]{:S(2)}) collective-permute-start(bf16[80,4608]{1,0:T(8,128)(2,1)} %get-tuple-element.67), channel_id=1, source_target_pairs={{0,24},{8,16},{16,8},{24,0},{1,25},{9,17},{17,9},{25,1},{2,26},{10... | collective-permute-start | bytes 2211848 | tf_op jit(solution)/shard_map/ppermute | solution.py:16
  225.7 42.9 %collective-permute-start.19 = (bf16[64,4608]{1,0:T(8,128)(2,1)}, bf16[64,4608]{1,0:T(8,128)(2,1)}, u32[]{:S(2)}, u32[]{:S(2)}) collective-permute-start(bf16[64,4608]{1,0:T(8,128)(2,1)} %get-tuple-element.68), channel_id=1, source_target_pairs={{0,24},{8,16},{16,8},{24,0},{1,25},{9,17},{17,9},{25,1},{2,26},{10... | collective-permute-start | bytes 1769480 | tf_op jit(solution)/shard_map/ppermute | solution.py:16
  323.1 50.5 %collective-permute-start.30 = (bf16[192,576]{1,0:T(8,128)(2,1)}, bf16[192,576]{1,0:T(8,128)(2,1)S(1)}, u32[]{:S(2)}, u32[]{:S(2)}) collective-permute-start(bf16[192,576]{1,0:T(8,128)(2,1)} %total.2.refs_0_), channel_id=1, source_target_pairs={{0,4},{2,6},{4,0},{6,2},{1,5},{3,7},{5,1},{7,3},{8,12},{10,14},{12... | collective-permute-start | bytes 663560 | tf_op jit(solution)/shard_map/ppermute | solution.py:16
  365.8 29.2 %collective-permute-start.31 = (bf16[192,576]{1,0:T(8,128)(2,1)S(1)}, bf16[192,576]{1,0:T(8,128)(2,1)S(1)}, u32[]{:S(2)}, u32[]{:S(2)}) collective-permute-start(bf16[192,576]{1,0:T(8,128)(2,1)S(1)} %copy-done), channel_id=1, source_target_pairs={{2,4},{4,2},{3,5},{5,3},{10,12},{12,10},{11,13},{13,11},{18,20},{2... | collective-permute-start | bytes 663560 | tf_op jit(solution)/shard_map/ppermute | solution.py:24
  366.5 28.6 %collective-permute-start.29 = (bf16[192,576]{1,0:T(8,128)(2,1)S(1)}, bf16[192,576]{1,0:T(8,128)(2,1)S(1)}, u32[]{:S(2)}, u32[]{:S(2)}) collective-permute-start(bf16[192,576]{1,0:T(8,128)(2,1)S(1)} %copy-done), channel_id=1, source_target_pairs={{0,2},{2,0},{4,6},{6,4},{1,3},{3,1},{5,7},{7,5},{8,10},{10,8},{12,... | collective-permute-start | bytes 663560 | tf_op jit(solution)/shard_map/ppermute | solution.py:16
  (132 other events, 3003.3 us)

commit v3 on v2

v3 whole, which is shorter than its diff:
```python
import functools
import math

import jax
import jax.numpy as jnp
from jax import lax
from jax.experimental import pallas as pl
from jax.experimental.pallas import tpu as pltpu
from jax.sharding import Mesh, PartitionSpec as P


SHARES = (4, 4, 4, 2, 2)
GROUPS = ((0, 1, 2), (3, 4))


def swap(value, axis, offset):
    return lax.ppermute(value, axis, [(i, i ^ offset) for i in range(lax.axis_size(axis))])


def spread_first(value, axis):
    size = lax.axis_size(axis)
    if size != 4:
        return [value] + [swap(value, axis, k) for k in range(1, size)]
    middle = lax.ppermute(value, axis, [(1, 2), (2, 1)])
    far = lax.ppermute(value, axis, [(0, 2), (3, 1)])
    return [value, lax.ppermute(value, axis, [(i, i ^ 1) for i in range(size)]), far, middle]


def spread_last(blocks, axis):
    if lax.axis_size(axis) != 4:
        return blocks
    ends = [(1, 0), (2, 3)]
    return list(blocks) + [lax.ppermute(blocks[3], axis, ends), lax.ppermute(blocks[2], axis, ends)]


def spread_small(value, axis):
    size = lax.axis_size(axis)
    near, *rest = [swap(value, axis, k) for k in range(1, size if size != 4 else 3)]
    if size != 4:
        return [value, near] + rest
    middle = lax.ppermute(value, axis, [(1, 2), (2, 1)])
    return [value, near] + rest + [middle, lax.ppermute(rest[0], axis, [(1, 0), (2, 3)])]


def place(at, size, count, at_end):
    return jnp.where((at >= 2 * size - count) & (at_end == 1), at + count - size, at)


def order_kernel(size, by_ref, *refs):
    outs, (held, in_sems, out_sems) = refs[-size - 3 : -3], refs[-3:]
    blocks = refs[: -size - 3]
    for k in range(size):
        at = k ^ by_ref[0]
        at = place(at, size, len(blocks), by_ref[1])
        for b, block in enumerate(blocks):
            pl.when(at == b)(pltpu.make_async_copy(block, held.at[k], in_sems.at[k]).start)
    for k in range(size):
        pltpu.make_async_copy(blocks[0], held.at[k], in_sems.at[k]).wait()
        pltpu.make_async_copy(held.at[k], outs[k], out_sems.at[k]).start()
    for k in range(size):
        pltpu.make_async_copy(held.at[k], outs[k], out_sems.at[k]).wait()


def xor_order(blocks, by, axis):
    size, index = lax.axis_size(axis), lax.axis_index(axis)
    at_end = (index == 0) | (index == size - 1)
    rows, cols = blocks[0].shape
    dtype = blocks[0].dtype
    hbm = pl.BlockSpec(memory_space=pltpu.HBM)
    return pl.pallas_call(
        functools.partial(order_kernel, size),
        in_specs=[pl.BlockSpec(memory_space=pltpu.SMEM)] + [hbm] * len(blocks),
        out_specs=[hbm] * size,
        out_shape=[jax.ShapeDtypeStruct((rows, cols), dtype)] * size,
        scratch_shapes=[pltpu.VMEM((size, rows, cols), dtype), pltpu.SemaphoreType.DMA((size,)), pltpu.SemaphoreType.DMA((size,))],
        cost_estimate=pl.CostEstimate(flops=rows * cols * size, bytes_accessed=4 * rows * cols * size, transcendentals=0),
        name="order",
    )(jnp.stack([by, at_end.astype(jnp.int32)]), *blocks)


def product_kernel(count, subs, *refs):
    lefts, weights = refs[:count], refs[count : count + subs]
    keep, send, left, right, total = refs[count + subs :]
    step, toks = pl.program_id(0), 2 * keep.shape[1]
    n, cols = keep.shape[2:]
    at = 0
    for ref in lefts:
        left[at : at + ref.shape[0]] = ref[...]
        at += ref.shape[0]
    for k in range(subs):
        right[k * cols : (k + 1) * cols] = weights[k][...]
    term = contract_last(left[...], right[...])

    @pl.when(step == 0)
    def _():
        total[...] = term

    @pl.when(step > 0)
    def _():
        total[...] += term

    @pl.when(step == pl.num_programs(0) - 1)
    def _():
        for k in range(subs):
            for d in range(0, toks, 2):
                here = slice(k * cols, (k + 1) * cols)
                keep[k, d // 2] = total[d * n : (d + 1) * n, here]
                send[k, d // 2] = total[(d + 1) * n : (d + 2) * n, here].astype(send.dtype)


def product(lefts, weights):
    subs, toks = len(weights), len(lefts)
    cols, depth = weights[0].shape
    n = sum(piece.shape[0] for piece in lefts[0])
    rows = n * toks
    parts = 2 if rows <= 512 else 3
    tile = depth // parts if depth % (parts * 128) == 0 and depth > 2048 else depth
    flat = [piece for pieces in lefts for piece in pieces]
    shape = (subs, toks // 2, n, cols)
    return pl.pallas_call(
        functools.partial(product_kernel, len(flat), subs),
        grid=(depth // tile,),
        in_specs=[pl.BlockSpec((piece.shape[0], tile), lambda i: (0, i)) for piece in flat]
        + [pl.BlockSpec((cols, tile), lambda i: (0, i))] * subs,
        out_specs=[pl.BlockSpec(shape, lambda i: (0, 0, 0, 0))] * 2,
        out_shape=[jax.ShapeDtypeStruct(shape, jnp.float32), jax.ShapeDtypeStruct(shape, jnp.bfloat16)],
        scratch_shapes=[
            pltpu.VMEM((rows, tile), jnp.bfloat16),
            pltpu.VMEM((subs * cols, tile), jnp.bfloat16),
            pltpu.VMEM((rows, subs * cols), jnp.float32),
        ],
        cost_estimate=pl.CostEstimate(
            flops=2 * rows * cols * depth * subs, bytes_accessed=2 * depth * (rows + cols * subs), transcendentals=0
        ),
        name="product",
    )(*flat, *weights)


def pair_kernel(keep, arrived, *outs):
    half = keep.shape[1]
    for i, out in enumerate(outs):
        out[...] = (keep[i // half, i % half] + arrived[i // half, i % half].astype(jnp.float32)).astype(out.dtype)


def pair(keep, arrived):
    subs, half, n, cols = keep.shape
    outs = pl.pallas_call(
        pair_kernel,
        out_shape=[jax.ShapeDtypeStruct((n, cols), jnp.bfloat16 if i else jnp.float32) for i in range(subs * half)],
        cost_estimate=pl.CostEstimate(flops=keep.size, bytes_accessed=8 * keep.size, transcendentals=0),
        name="pair",
    )(keep, arrived)
    return [outs[k * half : (k + 1) * half] for k in range(subs)]


def total_kernel(*refs):
    total = refs[0][...]
    for ref in refs[1:-1]:
        total += ref[...].astype(jnp.float32)
    refs[-1][...] = total.astype(refs[-1].dtype)


def total_of(own, others):
    return pl.pallas_call(
        total_kernel,
        out_shape=jax.ShapeDtypeStruct(own.shape, jnp.bfloat16),
        cost_estimate=pl.CostEstimate(flops=own.size * len(others), bytes_accessed=2 * own.size * (len(others) + 3), transcendentals=0),
        name="total",
    )(own, *others)


def hessian_kernel(pieces, subs, scaling, sub_ref, *refs):
    out, refs = refs[-1], refs[:-1]

    def stacked(k):
        return jnp.concatenate([ref[...] for ref in refs[k * pieces : (k + 1) * pieces]], axis=0)

    left = stacked(0)
    cols = left.shape[1]
    for k in range(subs):
        term = contract_rows(left, stacked(k + 1)) * scaling
        for by in range(subs):

            @pl.when(sub_ref[0] == by)
            def _(k=k, by=by, term=term):
                out[:, (by ^ k) * cols : ((by ^ k) + 1) * cols] = term


def hessian_of(left, right, scaling, sub):
    subs, cols = len(right), left[0].shape[1]
    rows = sum(piece.shape[0] for piece in left)
    vmem = pl.BlockSpec(memory_space=pltpu.VMEM)
    return pl.pallas_call(
        functools.partial(hessian_kernel, len(left), subs, scaling),
        in_specs=[pl.BlockSpec(memory_space=pltpu.SMEM)] + [vmem] * (len(left) * (subs + 1)),
        out_specs=vmem,
        out_shape=jax.ShapeDtypeStruct((cols, subs * cols), jnp.float32),
        cost_estimate=pl.CostEstimate(flops=2 * rows * cols * cols * subs, bytes_accessed=4 * cols * cols * subs, transcendentals=0),
        name="hessian",
    )(sub.reshape(1), *left, *[piece for pieces in right for piece in pieces])


def pick_kernel(toks, subs, share, at_ref, *refs):
    outs, sems = refs[-subs - 1 : -1], refs[-1]
    groups, at = [], 0
    count = (len(refs) - subs - 1) // len(GROUPS)
    for g in range(len(GROUPS)):
        blocks = refs[g * count : (g + 1) * count]
        groups.append((at, blocks))
        at += blocks[0].shape[0]
    row, sub, at_end = at_ref[0], at_ref[1], at_ref[2]
    grain = math.gcd(share, *[blocks[0].shape[0] for _, blocks in groups])
    for k in range(subs):
        for q in range(toks):
            b = place(q ^ row, toks, count, at_end)
            for piece in range(0, share, grain):
                first = (row * subs + (sub ^ k)) * share + piece
                for start, blocks in groups:
                    for i, block in enumerate(blocks):

                        @pl.when((b == i) & (first >= start) & (first < start + block.shape[0]))
                        def _(k=k, q=q, block=block, first=first, start=start, piece=piece):
                            rows = block.at[pl.ds(pl.multiple_of(first - start, grain), grain)]
                            pltpu.make_async_copy(rows, outs[k].at[q, pl.ds(piece, grain)], sems.at[k, q]).start()

    for k in range(subs):
        for q in range(toks):
            pltpu.make_async_copy(refs[0].at[pl.ds(0, share)], outs[k].at[q], sems.at[k, q]).wait()


def pick(layer_rows, share, subs):
    toks, row = lax.axis_size("row"), lax.axis_index("row")
    cols = layer_rows[0][0].shape[1]
    flat = [block for blocks in layer_rows for block in blocks]
    at_end = ((row == 0) | (row == toks - 1)).astype(jnp.int32)
    return pl.pallas_call(
        functools.partial(pick_kernel, toks, subs, share),
        in_specs=[pl.BlockSpec(memory_space=pltpu.SMEM)] + [pl.BlockSpec(memory_space=pltpu.HBM)] * len(flat),
        out_specs=[pl.BlockSpec(memory_space=pltpu.VMEM)] * subs,
        out_shape=[jax.ShapeDtypeStruct((toks, share, cols), flat[0].dtype)] * subs,
        scratch_shapes=[pltpu.SemaphoreType.DMA((subs, toks))],
        cost_estimate=pl.CostEstimate(flops=0, bytes_accessed=4 * subs * toks * share * cols, transcendentals=0),
        name="pick",
    )(jnp.stack([row, lax.axis_index("sub"), at_end]), *flat)


def select_order(blocks, by):
    size = len(blocks)
    bit = 1
    while bit < size:
        flip = jnp.broadcast_to((by & bit) != 0, blocks[0].shape)
        blocks = [lax.select(flip, blocks[k ^ bit], blocks[k]) for k in range(size)]
        bit *= 2
    return blocks


def turn(blocks, axis):
    return list(blocks[:1]) + [swap(blocks[k], axis, k) for k in range(1, len(blocks))]


def contract_last(left, right):
    return lax.dot_general(left, right, (((1,), (1,)), ((), ())), preferred_element_type=jnp.float32)


def contract_rows(left, right):
    return lax.dot_general(left, right, (((0,), (0,)), ((), ())), preferred_element_type=jnp.float32)


def body(hidden_in, down_weight, keep_mask):
    tok, row, sub = lax.axis_index("tok"), lax.axis_index("row"), lax.axis_index("sub")
    toks, subs = lax.axis_size("tok"), lax.axis_size("sub")
    rows, depth = hidden_in.shape
    cols = down_weight.shape[0]
    steps = [rows * share // sum(SHARES) for share in SHARES]
    starts = [sum(steps[:j]) for j in range(len(steps))]

    def pruned(weight, mask, block):
        w = lax.dynamic_slice(weight, (0, block * depth), (cols, depth))
        return w * lax.dynamic_slice(mask, (0, block * depth), (cols, depth)).astype(w.dtype)

    pieces = [lax.optimization_barrier(hidden_in[at : at + n]) for at, n in zip(starts, steps)]
    seen = [spread_first(piece, "row") for piece in pieces]

    sent = [swap(pruned(down_weight, keep_mask, sub ^ k), "sub", k) for k in range(1, subs)]
    weight, mask, _ = lax.optimization_barrier((down_weight, keep_mask, seen[0][1]))
    kept, second = lax.optimization_barrier((pruned(weight, mask, sub), seen[1][2]))
    seen[1][2] = second
    weights = [kept] + sent

    arrived = []
    for j in range(len(steps)):
        blocks = spread_last(seen[j], "row")
        blocks = xor_order(blocks, tok ^ row, "row")
        arrived.append(turn(blocks, "tok"))

    def across(value, d, k):
        pairs = [(t * subs + s, (t ^ d) * subs + (s ^ k)) for t in range(toks) for s in range(subs)]
        return lax.ppermute(value, ("tok", "sub"), pairs) if d or k else value

    left, right, layer_rows = [], [[] for _ in range(subs)], []
    scaling = 2.0 / (rows * toks)
    for group in GROUPS:
        lefts = [[arrived[j][d] for j in group] for d in range(toks)]
        keep, send = product(lefts, weights)
        send = swap(send, "tok", 1)
        terms = pair(keep, send)
        others = [across(terms[k][d // 2], d, k) for k in range(subs) for d in range(0, toks, 2) if d or k]
        layer = total_of(terms[0][0], others)
        blocks = spread_small(layer, "row")
        layer_rows.append(blocks)
        mine = xor_order(blocks, tok ^ row, "row")
        left += turn([layer] * toks, "tok")
        for k in range(subs):
            right[k] += [across(mine[d], d, k) for d in range(toks)]
    hessian = hessian_of(left, right, scaling, sub)

    share = rows // (toks * subs)
    pieces = pick(layer_rows, share, subs)
    pieces = list(pieces[:1]) + [swap(pieces[k], "sub", k) for k in range(1, subs)]
    layer_out = jnp.stack(select_order(pieces, sub), axis=1).transpose(2, 0, 1, 3).reshape(share, toks * subs * cols)
    return layer_out, hessian


def solution(mesh):
    toks, both = mesh.shape["tok"], mesh.shape["col"]
    subs = both // toks
    grid = Mesh(mesh.devices.reshape(toks, toks, subs), ("tok", "row", "sub"))
    col = ("row", "sub")
    in_specs = (P("tok", col), P(col, "tok"), P(col, "tok"))
    out_specs = (P(("tok",) + col, None), P(col, "tok"))
    return jax.shard_map(body, mesh=grid, in_specs=in_specs, out_specs=out_specs, check_vma=False)
```

time: 459 us -> 445 us (0.969)
  Pallas kernels: 71.9 us -> 61.8 us
  local copies, waits for them, and re-layouts: 5.8 us -> 14.6 us
  waiting for transfers between devices: 255 us -> 248 us
  starting transfers between devices: 102 us -> 96.7 us
    ppermute x37 -> x29, waiting for transfers between devices: 193 us -> 81.5 us  [swap(): lax.ppermute(value, axis, [(i, i ^ offset) for i in range(lax.axis_size(a...]
    ppermute x14 -> x29, waiting for transfers between devices: 33.1 us -> 132 us  [the longest x5 46.3 us: spread_last(): lax.ppermute(blocks[2], axis, ends)]
    ppermute x14 -> x29, starting transfers between devices: 13.9 us -> 50.1 us  [the longest x5 20.3 us: spread_first(): far = lax.ppermute(value, axis, [(0, 2), (3, 1)])]
    ppermute x37 -> x29, starting transfers between devices: 60.4 us -> 28.2 us  [swap(): lax.ppermute(value, axis, [(i, i ^ offset) for i in range(lax.axis_size(a...]
    ppermute x28 -> x20, starting transfers between devices: 28 us -> 18.4 us  [across(): return lax.ppermute(value, ('tok', 'sub'), pairs) if d or k else value]
    pallas_call x6 -> x5, Pallas kernels: 44.7 us -> 35.3 us  [the longest x2 23.6 us: product(): pl.pallas_call(functools.partial(product_kernel, len(flat), subs), grid=(...]
    unnamed x154 -> x138, local copies, waits for them, and re-layouts: 4.33 us -> 11.6 us
    ppermute x28 -> x20, waiting for transfers between devices: 28.6 us -> 34.3 us  [across(): return lax.ppermute(value, ('tok', 'sub'), pairs) if d or k else value]
  transfers between devices with their start and end apart: 79 -> 78, of which waited for: 29 -> 35; matrix products, arithmetic and copies ran while one was open for 3% -> 3% of each run, Pallas kernels for 15% -> 12%
where the time goes in v3:
time: 445 us; the launch traced here: 444 us
  waiting for transfers between devices  248 us (56%)
  starting transfers between devices  96.7 us (22%)
  Pallas kernels  61.8 us (14%)
  other arithmetic  21.5 us (5%)
  local copies, waits for them, and re-layouts  14.6 us (3%)
    ppermute x29, waiting for transfers between devices, swap(): lax.ppermute(value, axis, [(i, i ^ offset) for i in range(lax.axis_size(a...  81.5 us
    ppermute x5, waiting for transfers between devices, spread_last(): lax.ppermute(blocks[2], axis, ends)  46.3 us
    ppermute x5, waiting for transfers between devices, spread_first(): far = lax.ppermute(value, axis, [(0, 2), (3, 1)])  44.5 us
    ppermute x20, waiting for transfers between devices, across(): return lax.ppermute(value, ('tok', 'sub'), pairs) if d or k else value  34.3 us
    ppermute x5, waiting for transfers between devices, spread_last(): lax.ppermute(blocks[3], axis, ends)  31.9 us
    ppermute x29, starting transfers between devices, swap(): lax.ppermute(value, axis, [(i, i ^ offset) for i in range(lax.axis_size(a...  28.2 us
    pallas_call x2, Pallas kernels, product(): pl.pallas_call(functools.partial(product_kernel, len(flat), subs), grid=(...  23.6 us
    ppermute x5, starting transfers between devices, spread_first(): far = lax.ppermute(value, axis, [(0, 2), (3, 1)])  20.3 us
  transfers between devices with their start and end apart: 78, of which 35 were waited for; matrix products, arithmetic and copies ran while one was open for 3% of the time, Pallas kernels for 12%

profile of v3, /device:TPU:0, one launch (start us, length us, event | category | flops | bytes accessed | tf_op | source)
XLA Modules:
  0.0 444.2 jit_solution(1359393286930201839)
XLA Ops:
  0.7 9.6 %fusion.1 = bf16[576,4608]{1,0:T(8,128)(2,1)} fusion(s32[576,9216]{1,0:T(8,128)} %param.5, s32[]{:T(128)S(6)} %select_n.15, bf16[576,9216]{1,0:T(8,128)(2,1)} %param.4), kind=kLoop, calls=%fused_computation.3 | loop fusion | flops 13271040 | bytes 21233668 | tf_op jit(solution)/shard_map/mul | solution.py:279
  22.6 17.5 %collective-permute-done.34.refs_2_ = bf16[32,4608]{1,0:T(8,128)(2,1)S(1)} collective-permute-done((bf16[32,4608]{1,0:T(8,128)(2,1)S(1)}, bf16[32,4608]{1,0:T(8,128)(2,1)S(1)}, u32[]{:S(2)}, u32[]{:S(2)}) %collective-permute-start.34) | collective-permute-done | bytes 294944 | tf_op jit(solution)/shard_map/ppermute | solution.py:25
  54.3 22.1 %collective-permute-done.39.refs_2_ = bf16[32,4608]{1,0:T(8,128)(2,1)S(1)} collective-permute-done((bf16[32,4608]{1,0:T(8,128)(2,1)}, bf16[32,4608]{1,0:T(8,128)(2,1)S(1)}, u32[]{:S(2)}, u32[]{:S(2)}) %collective-permute-start.39) | collective-permute-done | bytes 294944 | tf_op jit(solution)/shard_map/ppermute | solution.py:25
  78.0 7.0 %collective-permute-start.1 = (bf16[64,4608]{1,0:T(8,128)(2,1)S(1)}, bf16[64,4608]{1,0:T(8,128)(2,1)}, u32[]{:S(2)}, u32[]{:S(2)}) collective-permute-start(bf16[64,4608]{1,0:T(8,128)(2,1)S(1)} %get-tuple-element.98.refs_0_), channel_id=1, source_target_pairs={{0,4},{6,2},{1,5},{7,3},{8,12},{14,10},{9,13},{15,11},{16,20},{22,... | collective-permute-start | bytes 1769480 | tf_op jit(solution)/shard_map/ppermute | solution.py:25
  88.9 9.6 %fusion.refs_12_.refs_8_ = bf16[576,4608]{1,0:T(8,128)(2,1)} fusion(s32[576,9216]{1,0:T(8,128)} %param.5, s32[]{:T(128)S(6)} %select_n.14, bf16[576,9216]{1,0:T(8,128)(2,1)} %param.4), kind=kLoop, calls=%fused_computation.2 | loop fusion | flops 13271040 | bytes 21233668 | tf_op jit(solution)/shard_map/mul | solution.py:279
  109.3 28.5 %collective-permute-done.9.refs_5_ = bf16[64,4608]{1,0:T(8,128)(2,1)} collective-permute-done((bf16[64,4608]{1,0:T(8,128)(2,1)S(1)}, bf16[64,4608]{1,0:T(8,128)(2,1)}, u32[]{:S(2)}, u32[]{:S(2)}) %collective-permute-start.9) | collective-permute-done | bytes 589856 | tf_op jit(solution)/shard_map/ppermute | solution.py:33
  137.8 12.6 %collective-permute-done.8.refs_4_ = bf16[64,4608]{1,0:T(8,128)(2,1)} collective-permute-done((bf16[64,4608]{1,0:T(8,128)(2,1)}, bf16[64,4608]{1,0:T(8,128)(2,1)}, u32[]{:S(2)}, u32[]{:S(2)}) %collective-permute-start.8) | collective-permute-done | bytes 589856 | tf_op jit(solution)/shard_map/ppermute | solution.py:33
  154.9 8.0 %collective-permute-done.3.refs_4_ = bf16[64,4608]{1,0:T(8,128)(2,1)S(1)} collective-permute-done((bf16[64,4608]{1,0:T(8,128)(2,1)}, bf16[64,4608]{1,0:T(8,128)(2,1)S(1)}, u32[]{:S(2)}, u32[]{:S(2)}) %collective-permute-start.3) | collective-permute-done | bytes 589856 | tf_op jit(solution)/shard_map/ppermute | solution.py:33
  164.2 11.3 %collective-permute-done.4.refs_5_ = bf16[64,4608]{1,0:T(8,128)(2,1)S(1)} collective-permute-done((bf16[64,4608]{1,0:T(8,128)(2,1)}, bf16[64,4608]{1,0:T(8,128)(2,1)S(1)}, u32[]{:S(2)}, u32[]{:S(2)}) %collective-permute-start.4) | collective-permute-done | bytes 589856 | tf_op jit(solution)/shard_map/ppermute | solution.py:33
  179.6 8.6 %collective-permute-done.10.refs_1_ = bf16[64,4608]{1,0:T(8,128)(2,1)S(1)} collective-permute-done((bf16[64,4608]{1,0:T(8,128)(2,1)S(1)}, bf16[64,4608]{1,0:T(8,128)(2,1)S(1)}, u32[]{:S(2)}, u32[]{:S(2)}) %collective-permute-start.10) | collective-permute-done | bytes 589856 | tf_op jit(solution)/shard_map/ppermute | solution.py:26
  189.7 11.3 %collective-permute-done.13.refs_4_ = bf16[64,4608]{1,0:T(8,128)(2,1)} collective-permute-done((bf16[64,4608]{1,0:T(8,128)(2,1)S(1)}, bf16[64,4608]{1,0:T(8,128)(2,1)}, u32[]{:S(2)}, u32[]{:S(2)}) %collective-permute-start.13) | collective-permute-done | bytes 589856 | tf_op jit(solution)/shard_map/ppermute | solution.py:33
  200.9 6.5 %collective-permute-done.14.refs_5_ = bf16[64,4608]{1,0:T(8,128)(2,1)} collective-permute-done((bf16[64,4608]{1,0:T(8,128)(2,1)S(1)}, bf16[64,4608]{1,0:T(8,128)(2,1)}, u32[]{:S(2)}, u32[]{:S(2)}) %collective-permute-start.14) | collective-permute-done | bytes 589856 | tf_op jit(solution)/shard_map/ppermute | solution.py:33
  218.3 11.2 %collective-permute-done.18.refs_6_ = bf16[64,4608]{1,0:T(8,128)(2,1)} collective-permute-done((bf16[64,4608]{1,0:T(8,128)(2,1)}, bf16[64,4608]{1,0:T(8,128)(2,1)}, u32[]{:S(2)}, u32[]{:S(2)}) %collective-permute-start.18) | collective-permute-done | bytes 589856 | tf_op jit(solution)/shard_map/ppermute | solution.py:17
  230.4 11.6 %collective-permute-done.21.refs_9_ = bf16[64,4608]{1,0:T(8,128)(2,1)S(1)} collective-permute-done((bf16[64,4608]{1,0:T(8,128)(2,1)}, bf16[64,4608]{1,0:T(8,128)(2,1)S(1)}, u32[]{:S(2)}, u32[]{:S(2)}) %collective-permute-start.21) | collective-permute-done | bytes 589856 | tf_op jit(solution)/shard_map/ppermute | solution.py:17
  244.1 10.6 %collective-permute-done.20.refs_8_ = bf16[64,4608]{1,0:T(8,128)(2,1)S(1)} collective-permute-done((bf16[64,4608]{1,0:T(8,128)(2,1)}, bf16[64,4608]{1,0:T(8,128)(2,1)S(1)}, u32[]{:S(2)}, u32[]{:S(2)}) %collective-permute-start.20) | collective-permute-done | bytes 589856 | tf_op jit(solution)/shard_map/ppermute | solution.py:17
  256.0 11.3 %collective-permute-done.23.refs_11_ = bf16[64,4608]{1,0:T(8,128)(2,1)S(1)} collective-permute-done((bf16[64,4608]{1,0:T(8,128)(2,1)}, bf16[64,4608]{1,0:T(8,128)(2,1)S(1)}, u32[]{:S(2)}, u32[]{:S(2)}) %collective-permute-start.23) | collective-permute-done | bytes 589856 | tf_op jit(solution)/shard_map/ppermute | solution.py:17
  270.1 15.6 %product.2 = (f32[2,2,192,576]{3,2,1,0:T(8,128)}, bf16[2,2,192,576]{3,2,1,0:T(8,128)(2,1)}) custom-call(bf16[64,4608]{1,0:T(8,128)(2,1)} %get-tuple-element.48.refs_0_, bf16[64,4608]{1,0:T(8,128)(2,1)} %get-tuple-element.52.refs_1_, bf16[64,4608]{1,0:T(8,128)(2,1)} %get-tuple-element.53.refs_2_, bf16[64,4608]{1,0:T(8,128)(2,1)} %collective-permute-done.15.refs_3_, ...), custom_call_target="tpu_custom_call" | custom-call | flops 8153726976 | bytes 17694720 | tf_op jit(solution)/shard_map/product/pallas_call | solution.py:120
  298.6 6.3 %collective-permute-done.45.refs_4_ = bf16[32,4608]{1,0:T(8,128)(2,1)S(1)} collective-permute-done((bf16[32,4608]{1,0:T(8,128)(2,1)}, bf16[32,4608]{1,0:T(8,128)(2,1)S(1)}, u32[]{:S(2)}, u32[]{:S(2)}) %collective-permute-start.45) | collective-permute-done | bytes 294944 | tf_op jit(solution)/shard_map/ppermute | solution.py:17
  304.9 6.3 %collective-permute-done.46.refs_5_ = bf16[32,4608]{1,0:T(8,128)(2,1)S(1)} collective-permute-done((bf16[32,4608]{1,0:T(8,128)(2,1)}, bf16[32,4608]{1,0:T(8,128)(2,1)S(1)}, u32[]{:S(2)}, u32[]{:S(2)}) %collective-permute-start.46) | collective-permute-done | bytes 294944 | tf_op jit(solution)/shard_map/ppermute | solution.py:17
  315.9 6.3 %collective-permute-done.48.refs_7_ = bf16[32,4608]{1,0:T(8,128)(2,1)S(1)} collective-permute-done((bf16[32,4608]{1,0:T(8,128)(2,1)}, bf16[32,4608]{1,0:T(8,128)(2,1)S(1)}, u32[]{:S(2)}, u32[]{:S(2)}) %collective-permute-start.48) | collective-permute-done | bytes 294944 | tf_op jit(solution)/shard_map/ppermute | solution.py:17
  322.9 7.9 %product.3 = (f32[2,2,64,576]{3,2,1,0:T(8,128)}, bf16[2,2,64,576]{3,2,1,0:T(8,128)(2,1)}) custom-call(bf16[32,4608]{1,0:T(8,128)(2,1)} %get-tuple-element.70.refs_0_, bf16[32,4608]{1,0:T(8,128)(2,1)} %get-tuple-element.71.refs_1_, bf16[32,4608]{1,0:T(8,128)(2,1)} %copy-done.21, bf16[32,4608]{1,0:T(8,128)(2,1)} %copy-done.22, bf16[32,4608]{1,0:T(8,128)(2,1)} %copy-done.23, ...), custom_call_target="tpu_custom_call" | custom-call | flops 2717908992 | bytes 12976128 | tf_op jit(solution)/shard_map/product/pallas_call | solution.py:120
  421.7 6.2 %collective-permute-done.66.refs_11_ = bf16[192,576]{1,0:T(8,128)(2,1)S(1)} collective-permute-done((bf16[192,576]{1,0:T(8,128)(2,1)}, bf16[192,576]{1,0:T(8,128)(2,1)S(1)}, u32[]{:S(2)}, u32[]{:S(2)}) %collective-permute-start.66) | collective-permute-done | bytes 221216 | tf_op jit(solution)/shard_map/ppermute | solution.py:298
  427.9 7.8 %collective-permute-done.70.refs_16_ = bf16[192,576]{1,0:T(8,128)(2,1)S(1)} collective-permute-done((bf16[192,576]{1,0:T(8,128)(2,1)}, bf16[192,576]{1,0:T(8,128)(2,1)S(1)}, u32[]{:S(2)}, u32[]{:S(2)}) %collective-permute-start.70) | collective-permute-done | bytes 221216 | tf_op jit(solution)/shard_map/ppermute | solution.py:298
  437.2 7.0 %hessian.1 = f32[576,1152]{1,0:T(8,128)} custom-call(s32[1]{0:T(128)} %bitcast.1.sub_ref, bf16[192,576]{1,0:T(8,128)(2,1)} %total.2.refs_0_, bf16[192,576]{1,0:T(8,128)(2,1)} %copy-done.40, bf16[192,576]{1,0:T(8,128)(2,1)} %copy-done.41, bf16[192,576]{1,0:T(8,128)(2,1)} %copy-done.42, bf16[64,576]{1,0:T(8,128)(2,1)} %total.3.refs_5_.refs_0_.refs_4_, ...), custom_call_target="tpu_custom_call" | custom-call | flops 1358954496 | bytes 2654208 | tf_op jit(solution)/shard_map/hessian/pallas_call | solution.py:193
  (295 shorter events, 182.1 us)
Async XLA Ops:
  10.2 258.4 %collective-permute-start.24 = (bf16[576,4608]{1,0:T(8,128)(2,1)}, bf16[576,4608]{1,0:T(8,128)(2,1)}, u32[]{:S(2)}, u32[]{:S(2)}) collective-permute-start(bf16[576,4608]{1,0:T(8,128)(2,1)} %fusion.1), channel_id=1, source_target_pairs={{0,1},{1,0},{2,3},{3,2},{4,5},{5,4},{6,7},{7,6},{8,9},{9,8},{10,11... | collective-permute-start | bytes 15925256 | tf_op jit(solution)/shard_map/ppermute | solution.py:17
  15.6 35.7 %collective-permute-start = (bf16[64,4608]{1,0:T(8,128)(2,1)S(1)}, bf16[64,4608]{1,0:T(8,128)(2,1)S(1)}, u32[]{:S(2)}, u32[]{:S(2)}) collective-permute-start(bf16[64,4608]{1,0:T(8,128)(2,1)S(1)} %get-tuple-element.98.refs_0_), channel_id=1, source_target_pairs={{0,2},{2,0},{4,6},{6,4},{1,3},{3,1},{5,7},{7,5},{8,10},{10,8},{12,... | collective-permute-start | bytes 1769480 | tf_op jit(solution)/shard_map/ppermute | solution.py:26
  21.9 26.0 %collective-permute-start.40 = (bf16[32,4608]{1,0:T(8,128)(2,1)}, bf16[32,4608]{1,0:T(8,128)(2,1)S(1)}, u32[]{:S(2)}, u32[]{:S(2)}) collective-permute-start(bf16[32,4608]{1,0:T(8,128)(2,1)} %get-tuple-element.94.refs_0_), channel_id=1, source_target_pairs={{2,4},{4,2},{3,5},{5,3},{10,12},{12,10},{11,13},{13,11},{18,20},{2... | collective-permute-start | bytes 884744 | tf_op jit(solution)/shard_map/ppermute | solution.py:24
  40.1 37.9 %collective-permute-start.6 = (bf16[64,4608]{1,0:T(8,128)(2,1)}, bf16[64,4608]{1,0:T(8,128)(2,1)S(1)}, u32[]{:S(2)}, u32[]{:S(2)}) collective-permute-start(bf16[64,4608]{1,0:T(8,128)(2,1)} %get-tuple-element.97.refs_0_), channel_id=1, source_target_pairs={{0,4},{6,2},{1,5},{7,3},{8,12},{14,10},{9,13},{15,11},{16,20},{22,... | collective-permute-start | bytes 1769480 | tf_op jit(solution)/shard_map/ppermute | solution.py:25
  46.4 38.5 %collective-permute-start.7 = (bf16[64,4608]{1,0:T(8,128)(2,1)}, bf16[64,4608]{1,0:T(8,128)(2,1)}, u32[]{:S(2)}, u32[]{:S(2)}) collective-permute-start(bf16[64,4608]{1,0:T(8,128)(2,1)} %get-tuple-element.97.refs_0_), channel_id=1, source_target_pairs={{2,4},{4,2},{3,5},{5,3},{10,12},{12,10},{11,13},{13,11},{18,20},{2... | collective-permute-start | bytes 1769480 | tf_op jit(solution)/shard_map/ppermute | solution.py:24
  47.9 37.7 %collective-permute-start.5 = (bf16[64,4608]{1,0:T(8,128)(2,1)}, bf16[64,4608]{1,0:T(8,128)(2,1)}, u32[]{:S(2)}, u32[]{:S(2)}) collective-permute-start(bf16[64,4608]{1,0:T(8,128)(2,1)} %get-tuple-element.97.refs_0_), channel_id=1, source_target_pairs={{0,2},{2,0},{4,6},{6,4},{1,3},{3,1},{5,7},{7,5},{8,10},{10,8},{12,... | collective-permute-start | bytes 1769480 | tf_op jit(solution)/shard_map/ppermute | solution.py:26
  98.5 39.2 %collective-permute-start.9 = (bf16[64,4608]{1,0:T(8,128)(2,1)S(1)}, bf16[64,4608]{1,0:T(8,128)(2,1)}, u32[]{:S(2)}, u32[]{:S(2)}) collective-permute-start(bf16[64,4608]{1,0:T(8,128)(2,1)S(1)} %collective-permute-done.6.refs_2_), channel_id=1, source_target_pairs={{2,0},{4,6},{3,1},{5,7},{10,8},{12,14},{11,9},{13,15},{18,16},{20,... | collective-permute-start | bytes 1769480 | tf_op jit(solution)/shard_map/ppermute | solution.py:33
  99.9 50.5 %collective-permute-start.8 = (bf16[64,4608]{1,0:T(8,128)(2,1)}, bf16[64,4608]{1,0:T(8,128)(2,1)}, u32[]{:S(2)}, u32[]{:S(2)}) collective-permute-start(bf16[64,4608]{1,0:T(8,128)(2,1)} %collective-permute-done.7.refs_3_), channel_id=1, source_target_pairs={{2,0},{4,6},{3,1},{5,7},{10,8},{12,14},{11,9},{13,15},{18,16},{20,... | collective-permute-start | bytes 1769480 | tf_op jit(solution)/shard_map/ppermute | solution.py:33
  101.2 61.7 %collective-permute-start.3 = (bf16[64,4608]{1,0:T(8,128)(2,1)}, bf16[64,4608]{1,0:T(8,128)(2,1)S(1)}, u32[]{:S(2)}, u32[]{:S(2)}) collective-permute-start(bf16[64,4608]{1,0:T(8,128)(2,1)} %collective-permute-done.2.refs_3_), channel_id=1, source_target_pairs={{2,0},{4,6},{3,1},{5,7},{10,8},{12,14},{11,9},{13,15},{18,16},{20,... | collective-permute-start | bytes 1769480 | tf_op jit(solution)/shard_map/ppermute | solution.py:33
  107.3 68.2 %collective-permute-start.4 = (bf16[64,4608]{1,0:T(8,128)(2,1)}, bf16[64,4608]{1,0:T(8,128)(2,1)S(1)}, u32[]{:S(2)}, u32[]{:S(2)}) collective-permute-start(bf16[64,4608]{1,0:T(8,128)(2,1)} %collective-permute-done.1.refs_2_), channel_id=1, source_target_pairs={{2,0},{4,6},{3,1},{5,7},{10,8},{12,14},{11,9},{13,15},{18,16},{20,... | collective-permute-start | bytes 1769480 | tf_op jit(solution)/shard_map/ppermute | solution.py:33
  137.7 50.5 %collective-permute-start.10 = (bf16[64,4608]{1,0:T(8,128)(2,1)S(1)}, bf16[64,4608]{1,0:T(8,128)(2,1)S(1)}, u32[]{:S(2)}, u32[]{:S(2)}) collective-permute-start(bf16[64,4608]{1,0:T(8,128)(2,1)S(1)} %get-tuple-element.96.refs_0_), channel_id=1, source_target_pairs={{0,2},{2,0},{4,6},{6,4},{1,3},{3,1},{5,7},{7,5},{8,10},{10,8},{12,... | collective-permute-start | bytes 1769480 | tf_op jit(solution)/shard_map/ppermute | solution.py:26
  150.4 50.6 %collective-permute-start.13 = (bf16[64,4608]{1,0:T(8,128)(2,1)S(1)}, bf16[64,4608]{1,0:T(8,128)(2,1)}, u32[]{:S(2)}, u32[]{:S(2)}) collective-permute-start(bf16[64,4608]{1,0:T(8,128)(2,1)S(1)} %collective-permute-done.12.refs_3_), channel_id=1, source_target_pairs={{2,0},{4,6},{3,1},{5,7},{10,8},{12,14},{11,9},{13,15},{18,16},{20,... | collective-permute-start | bytes 1769480 | tf_op jit(solution)/shard_map/ppermute | solution.py:33
  162.9 44.5 %collective-permute-start.14 = (bf16[64,4608]{1,0:T(8,128)(2,1)S(1)}, bf16[64,4608]{1,0:T(8,128)(2,1)}, u32[]{:S(2)}, u32[]{:S(2)}) collective-permute-start(bf16[64,4608]{1,0:T(8,128)(2,1)S(1)} %collective-permute-done.11.refs_2_), channel_id=1, source_target_pairs={{2,0},{4,6},{3,1},{5,7},{10,8},{12,14},{11,9},{13,15},{18,16},{20,... | collective-permute-start | bytes 1769480 | tf_op jit(solution)/shard_map/ppermute | solution.py:33
  175.6 31.9 %collective-permute-start.16 = (bf16[64,4608]{1,0:T(8,128)(2,1)}, bf16[64,4608]{1,0:T(8,128)(2,1)}, u32[]{:S(2)}, u32[]{:S(2)}) collective-permute-start(bf16[64,4608]{1,0:T(8,128)(2,1)} %get-tuple-element.55), channel_id=1, source_target_pairs={{0,8},{8,0},{16,24},{24,16},{1,9},{9,1},{17,25},{25,17},{2,10},{10... | collective-permute-start | bytes 1769480 | tf_op jit(solution)/shard_map/ppermute | solution.py:17
  212.2 29.8 %collective-permute-start.21 = (bf16[64,4608]{1,0:T(8,128)(2,1)}, bf16[64,4608]{1,0:T(8,128)(2,1)S(1)}, u32[]{:S(2)}, u32[]{:S(2)}) collective-permute-start(bf16[64,4608]{1,0:T(8,128)(2,1)} %get-tuple-element.60), channel_id=1, source_target_pairs={{0,24},{8,16},{16,8},{24,0},{1,25},{9,17},{17,9},{25,1},{2,26},{10... | collective-permute-start | bytes 1769480 | tf_op jit(solution)/shard_map/ppermute | solution.py:17
  216.7 26.1 %collective-permute-start.17 = (bf16[64,4608]{1,0:T(8,128)(2,1)}, bf16[64,4608]{1,0:T(8,128)(2,1)S(1)}, u32[]{:S(2)}, u32[]{:S(2)}) collective-permute-start(bf16[64,4608]{1,0:T(8,128)(2,1)} %get-tuple-element.56), channel_id=1, source_target_pairs={{0,8},{8,0},{16,24},{24,16},{1,9},{9,1},{17,25},{25,17},{2,10},{10... | collective-permute-start | bytes 1769480 | tf_op jit(solution)/shard_map/ppermute | solution.py:17
  216.9 37.9 %collective-permute-start.20 = (bf16[64,4608]{1,0:T(8,128)(2,1)}, bf16[64,4608]{1,0:T(8,128)(2,1)S(1)}, u32[]{:S(2)}, u32[]{:S(2)}) collective-permute-start(bf16[64,4608]{1,0:T(8,128)(2,1)} %get-tuple-element.59), channel_id=1, source_target_pairs={{0,16},{8,24},{16,0},{24,8},{1,17},{9,25},{17,1},{25,9},{2,18},{10... | collective-permute-start | bytes 1769480 | tf_op jit(solution)/shard_map/ppermute | solution.py:17
  229.6 37.7 %collective-permute-start.23 = (bf16[64,4608]{1,0:T(8,128)(2,1)}, bf16[64,4608]{1,0:T(8,128)(2,1)S(1)}, u32[]{:S(2)}, u32[]{:S(2)}) collective-permute-start(bf16[64,4608]{1,0:T(8,128)(2,1)} %get-tuple-element.62), channel_id=1, source_target_pairs={{0,24},{8,16},{16,8},{24,0},{1,25},{9,17},{17,9},{25,1},{2,26},{10... | collective-permute-start | bytes 1769480 | tf_op jit(solution)/shard_map/ppermute | solution.py:17
  242.0 48.1 %collective-permute-start.38 = (bf16[32,4608]{1,0:T(8,128)(2,1)}, bf16[32,4608]{1,0:T(8,128)(2,1)S(1)}, u32[]{:S(2)}, u32[]{:S(2)}) collective-permute-start(bf16[32,4608]{1,0:T(8,128)(2,1)} %get-tuple-element.94.refs_0_), channel_id=1, source_target_pairs={{0,2},{2,0},{4,6},{6,4},{1,3},{3,1},{5,7},{7,5},{8,10},{10,8},{12,... | collective-permute-start | bytes 884744 | tf_op jit(solution)/shard_map/ppermute | solution.py:26
  242.8 42.9 %collective-permute-start.36 = (bf16[32,4608]{1,0:T(8,128)(2,1)}, bf16[32,4608]{1,0:T(8,128)(2,1)S(1)}, u32[]{:S(2)}, u32[]{:S(2)}) collective-permute-start(bf16[32,4608]{1,0:T(8,128)(2,1)} %copy-done.27), channel_id=1, source_target_pairs={{2,0},{4,6},{3,1},{5,7},{10,8},{12,14},{11,9},{13,15},{18,16},{20,... | collective-permute-start | bytes 884744 | tf_op jit(solution)/shard_map/ppermute | solution.py:33
  254.7 31.2 %collective-permute-start.37 = (bf16[32,4608]{1,0:T(8,128)(2,1)}, bf16[32,4608]{1,0:T(8,128)(2,1)S(1)}, u32[]{:S(2)}, u32[]{:S(2)}) collective-permute-start(bf16[32,4608]{1,0:T(8,128)(2,1)} %copy-done.29), channel_id=1, source_target_pairs={{2,0},{4,6},{3,1},{5,7},{10,8},{12,14},{11,9},{13,15},{18,16},{20,... | collective-permute-start | bytes 884744 | tf_op jit(solution)/shard_map/ppermute | solution.py:33
  285.8 45.7 %collective-permute-start.25 = (bf16[2,2,192,576]{3,2,1,0:T(8,128)(2,1)}, bf16[2,2,192,576]{3,2,1,0:T(8,128)(2,1)S(1)}, u32[]{:S(2)}, u32[]{:S(2)}) collective-permute-start(bf16[2,2,192,576]{3,2,1,0:T(8,128)(2,1)} %get-tuple-element.65), channel_id=1, source_target_pairs={{0,8},{8,0},{16,24},{24,16},{1,9},{9,1},{17,25},{25,17},{2,10},{10... | collective-permute-start | bytes 2654216 | tf_op jit(solution)/shard_map/ppermute | solution.py:17
  351.9 28.4 %collective-permute-start.30 = (bf16[192,576]{1,0:T(8,128)(2,1)}, bf16[192,576]{1,0:T(8,128)(2,1)S(1)}, u32[]{:S(2)}, u32[]{:S(2)}) collective-permute-start(bf16[192,576]{1,0:T(8,128)(2,1)} %total.2.refs_0_), channel_id=1, source_target_pairs={{0,4},{2,6},{4,0},{6,2},{1,5},{3,7},{5,1},{7,3},{8,12},{10,14},{12... | collective-permute-start | bytes 663560 | tf_op jit(solution)/shard_map/ppermute | solution.py:17
  409.2 26.4 %collective-permute-start.71 = (bf16[192,576]{1,0:T(8,128)(2,1)}, bf16[192,576]{1,0:T(8,128)(2,1)S(1)}, u32[]{:S(2)}, u32[]{:S(2)}) collective-permute-start(bf16[192,576]{1,0:T(8,128)(2,1)} %get-tuple-element.87), channel_id=1, source_target_pairs={{0,9},{1,8},{8,1},{9,0},{16,25},{17,24},{24,17},{25,16},{2,11},{3,... | collective-permute-start | bytes 663560 | tf_op jit(solution)/shard_map/ppermute | solution.py:298
  (123 other events, 2188.4 us)

commit v4 on v3

--- a/solution.py
+++ b/solution.py
@@ -9,7 +9,7 @@
 from jax.sharding import Mesh, PartitionSpec as P
 
 
-SHARES = (4, 4, 4, 2, 2)
+SHARES = (4, 4, 2, 4, 2)
 GROUPS = ((0, 1, 2), (3, 4))
 
 
@@ -283,9 +283,7 @@
 
     sent = [swap(pruned(down_weight, keep_mask, sub ^ k), "sub", k) for k in range(1, subs)]
     weight, mask, _ = lax.optimization_barrier((down_weight, keep_mask, seen[0][1]))
-    kept, second = lax.optimization_barrier((pruned(weight, mask, sub), seen[1][2]))
-    seen[1][2] = second
-    weights = [kept] + sent
+    weights = [pruned(weight, mask, sub)] + sent
 
     arrived = []
     for j in range(len(steps)):
@@ -310,8 +308,10 @@
         layer_rows.append(blocks)
         mine = xor_order(blocks, tok ^ row, "row")
         left += turn([layer] * toks, "tok")
-        for k in range(subs):
-            right[k] += [across(mine[d], d, k) for d in range(toks)]
+        mine = [across(mine[d], d, 0) for d in range(toks)]
+        right[0] += mine
+        for k in range(1, subs):
+            right[k] += [swap(mine[d], "sub", k) for d in range(toks)]
     hessian = hessian_of(left, right, scaling, sub)
 
     share = rows // (toks * subs)

time: 445 us -> 393 us (0.88)
  waiting for transfers between devices: 248 us -> 185 us
  starting transfers between devices: 96.7 us -> 109 us
    ppermute x5, waiting for transfers between devices: 44.5 us -> 0.01 us  [spread_first(): far = lax.ppermute(value, axis, [(0, 2), (3, 1)])]
    ppermute x20 -> x12, waiting for transfers between devices: 34.3 us -> 5.27 us  [across(): return lax.ppermute(value, ('tok', 'sub'), pairs) if d or k else value]
    ppermute x5, waiting for transfers between devices: 46.3 us -> 63.7 us  [spread_last(): lax.ppermute(blocks[2], axis, ends)]
    ppermute x5, waiting for transfers between devices: 9.58 us -> 22.9 us  [spread_first(): lax.ppermute(value, axis, [(i, i ^ 1) for i in range(size)])]
    ppermute x5, starting transfers between devices: 20.3 us -> 31.6 us  [spread_first(): far = lax.ppermute(value, axis, [(0, 2), (3, 1)])]
    ppermute x29 -> x37, waiting for transfers between devices: 81.5 us -> 70.4 us  [swap(): lax.ppermute(value, axis, [(i, i ^ offset) for i in range(lax.axis_size(a...]
    ppermute x5, waiting for transfers between devices: 31.9 us -> 22.3 us  [spread_last(): lax.ppermute(blocks[3], axis, ends)]
    ppermute x20 -> x12, starting transfers between devices: 18.4 us -> 9.96 us  [across(): return lax.ppermute(value, ('tok', 'sub'), pairs) if d or k else value]
  transfers between devices with their start and end apart: 78 -> 78, of which waited for: 35 -> 29; matrix products, arithmetic and copies ran while one was open for 3% -> 6% of each run, Pallas kernels for 12% -> 14%
where the time goes in v4:
time: 393 us; the launch traced here: 392 us
  waiting for transfers between devices  185 us (47%)
  starting transfers between devices  109 us (28%)
  Pallas kernels  62.2 us (16%)
  other arithmetic  21.4 us (5%)
  local copies, waits for them, and re-layouts  13.4 us (3%)
    ppermute x37, waiting for transfers between devices, swap(): lax.ppermute(value, axis, [(i, i ^ offset) for i in range(lax.axis_size(a...  70.4 us
    ppermute x5, waiting for transfers between devices, spread_last(): lax.ppermute(blocks[2], axis, ends)  63.7 us
    ppermute x5, starting transfers between devices, spread_first(): far = lax.ppermute(value, axis, [(0, 2), (3, 1)])  31.6 us
    ppermute x37, starting transfers between devices, swap(): lax.ppermute(value, axis, [(i, i ^ offset) for i in range(lax.axis_size(a...  31.3 us
    pallas_call x2, Pallas kernels, product(): pl.pallas_call(functools.partial(product_kernel, len(flat), subs), grid=(...  23.8 us
    ppermute x5, waiting for transfers between devices, spread_first(): lax.ppermute(value, axis, [(i, i ^ 1) for i in range(size)])  22.9 us
    ppermute x5, waiting for transfers between devices, spread_last(): lax.ppermute(blocks[3], axis, ends)  22.3 us
    pallas_call x7, Pallas kernels, xor_order(): pl.pallas_call(functools.partial(order_kernel, size), in_specs=[pl.BlockS...  20.3 us
  transfers between devices with their start and end apart: 78, of which 29 were waited for; matrix products, arithmetic and copies ran while one was open for 6% of the time, Pallas kernels for 14%

profile of v4, /device:TPU:0, one launch (start us, length us, event | category | flops | bytes accessed | tf_op | source)
XLA Modules:
  0.0 391.7 jit_solution(11353425970780433917)
XLA Ops:
  3.2 9.6 %fusion.1 = bf16[576,4608]{1,0:T(8,128)(2,1)} fusion(s32[576,9216]{1,0:T(8,128)} %param.5, s32[]{:T(128)S(6)} %select_n.15, bf16[576,9216]{1,0:T(8,128)(2,1)} %param.4), kind=kLoop, calls=%fused_computation.3 | loop fusion | flops 13271040 | bytes 21233668 | tf_op jit(solution)/shard_map/mul | solution.py:279
  15.8 6.2 %collective-permute-start.39 = (bf16[32,4608]{1,0:T(8,128)(2,1)}, bf16[32,4608]{1,0:T(8,128)(2,1)S(1)}, u32[]{:S(2)}, u32[]{:S(2)}) collective-permute-start(bf16[32,4608]{1,0:T(8,128)(2,1)} %get-tuple-element.90.refs_0_), channel_id=1, source_target_pairs={{0,4},{6,2},{1,5},{7,3},{8,12},{14,10},{9,13},{15,11},{16,20},{22,... | collective-permute-start | bytes 884744 | tf_op jit(solution)/shard_map/ppermute | solution.py:25
  23.6 7.3 %collective-permute-start.11 = (bf16[32,4608]{1,0:T(8,128)(2,1)}, bf16[32,4608]{1,0:T(8,128)(2,1)}, u32[]{:S(2)}, u32[]{:S(2)}) collective-permute-start(bf16[32,4608]{1,0:T(8,128)(2,1)} %get-tuple-element.91.refs_0_), channel_id=1, source_target_pairs={{0,4},{6,2},{1,5},{7,3},{8,12},{14,10},{9,13},{15,11},{16,20},{22,... | collective-permute-start | bytes 884744 | tf_op jit(solution)/shard_map/ppermute | solution.py:25
  36.0 5.4 %collective-permute-start.34 = (bf16[64,4608]{1,0:T(8,128)(2,1)S(1)}, bf16[64,4608]{1,0:T(8,128)(2,1)S(1)}, u32[]{:S(2)}, u32[]{:S(2)}) collective-permute-start(bf16[64,4608]{1,0:T(8,128)(2,1)S(1)} %get-tuple-element.92.refs_0_), channel_id=1, source_target_pairs={{0,4},{6,2},{1,5},{7,3},{8,12},{14,10},{9,13},{15,11},{16,20},{22,... | collective-permute-start | bytes 1769480 | tf_op jit(solution)/shard_map/ppermute | solution.py:25
  41.4 12.1 %collective-permute-start.33 = (bf16[64,4608]{1,0:T(8,128)(2,1)S(1)}, bf16[64,4608]{1,0:T(8,128)(2,1)S(1)}, u32[]{:S(2)}, u32[]{:S(2)}) collective-permute-start(bf16[64,4608]{1,0:T(8,128)(2,1)S(1)} %get-tuple-element.92.refs_0_), channel_id=1, source_target_pairs={{0,2},{2,0},{4,6},{6,4},{1,3},{3,1},{5,7},{7,5},{8,10},{10,8},{12,... | collective-permute-start | bytes 1769480 | tf_op jit(solution)/shard_map/ppermute | solution.py:26
  53.6 18.7 %collective-permute-done.10.refs_1_ = bf16[32,4608]{1,0:T(8,128)(2,1)S(1)} collective-permute-done((bf16[32,4608]{1,0:T(8,128)(2,1)}, bf16[32,4608]{1,0:T(8,128)(2,1)S(1)}, u32[]{:S(2)}, u32[]{:S(2)}) %collective-permute-start.10) | collective-permute-done | bytes 294944 | tf_op jit(solution)/shard_map/ppermute | solution.py:26
  85.6 15.2 %collective-permute-done.42.refs_5_ = bf16[32,4608]{1,0:T(8,128)(2,1)} collective-permute-done((bf16[32,4608]{1,0:T(8,128)(2,1)S(1)}, bf16[32,4608]{1,0:T(8,128)(2,1)}, u32[]{:S(2)}, u32[]{:S(2)}) %collective-permute-start.42) | collective-permute-done | bytes 294944 | tf_op jit(solution)/shard_map/ppermute | solution.py:33
  102.8 8.1 %collective-permute-start.6 = (bf16[64,4608]{1,0:T(8,128)(2,1)S(1)}, bf16[64,4608]{1,0:T(8,128)(2,1)}, u32[]{:S(2)}, u32[]{:S(2)}) collective-permute-start(bf16[64,4608]{1,0:T(8,128)(2,1)S(1)} %get-tuple-element.93.refs_0_), channel_id=1, source_target_pairs={{0,4},{6,2},{1,5},{7,3},{8,12},{14,10},{9,13},{15,11},{16,20},{22,... | collective-permute-start | bytes 1769480 | tf_op jit(solution)/shard_map/ppermute | solution.py:25
  117.1 12.2 %collective-permute-done.14.refs_5_ = bf16[32,4608]{1,0:T(8,128)(2,1)} collective-permute-done((bf16[32,4608]{1,0:T(8,128)(2,1)}, bf16[32,4608]{1,0:T(8,128)(2,1)}, u32[]{:S(2)}, u32[]{:S(2)}) %collective-permute-start.14) | collective-permute-done | bytes 294944 | tf_op jit(solution)/shard_map/ppermute | solution.py:33
  138.1 5.1 %collective-permute-done.20.refs_8_ = bf16[32,4608]{1,0:T(8,128)(2,1)S(1)} collective-permute-done((bf16[32,4608]{1,0:T(8,128)(2,1)}, bf16[32,4608]{1,0:T(8,128)(2,1)S(1)}, u32[]{:S(2)}, u32[]{:S(2)}) %collective-permute-start.20) | collective-permute-done | bytes 294944 | tf_op jit(solution)/shard_map/ppermute | solution.py:17
  144.4 5.9 %collective-permute-done.3.refs_4_ = bf16[64,4608]{1,0:T(8,128)(2,1)S(1)} collective-permute-done((bf16[64,4608]{1,0:T(8,128)(2,1)}, bf16[64,4608]{1,0:T(8,128)(2,1)S(1)}, u32[]{:S(2)}, u32[]{:S(2)}) %collective-permute-start.3) | collective-permute-done | bytes 589856 | tf_op jit(solution)/shard_map/ppermute | solution.py:33
  151.2 11.8 %collective-permute-done.4.refs_5_ = bf16[64,4608]{1,0:T(8,128)(2,1)S(1)} collective-permute-done((bf16[64,4608]{1,0:T(8,128)(2,1)}, bf16[64,4608]{1,0:T(8,128)(2,1)S(1)}, u32[]{:S(2)}, u32[]{:S(2)}) %collective-permute-start.4) | collective-permute-done | bytes 589856 | tf_op jit(solution)/shard_map/ppermute | solution.py:33
  169.9 5.9 %collective-permute-done.8.refs_4_ = bf16[64,4608]{1,0:T(8,128)(2,1)} collective-permute-done((bf16[64,4608]{1,0:T(8,128)(2,1)S(1)}, bf16[64,4608]{1,0:T(8,128)(2,1)}, u32[]{:S(2)}, u32[]{:S(2)}) %collective-permute-start.8) | collective-permute-done | bytes 589856 | tf_op jit(solution)/shard_map/ppermute | solution.py:33
  175.8 12.6 %collective-permute-done.9.refs_5_ = bf16[64,4608]{1,0:T(8,128)(2,1)} collective-permute-done((bf16[64,4608]{1,0:T(8,128)(2,1)}, bf16[64,4608]{1,0:T(8,128)(2,1)}, u32[]{:S(2)}, u32[]{:S(2)}) %collective-permute-start.9) | collective-permute-done | bytes 589856 | tf_op jit(solution)/shard_map/ppermute | solution.py:33
  193.1 7.9 %collective-permute-done.36.refs_4_ = bf16[64,4608]{1,0:T(8,128)(2,1)} collective-permute-done((bf16[64,4608]{1,0:T(8,128)(2,1)S(1)}, bf16[64,4608]{1,0:T(8,128)(2,1)}, u32[]{:S(2)}, u32[]{:S(2)}) %collective-permute-start.36) | collective-permute-done | bytes 589856 | tf_op jit(solution)/shard_map/ppermute | solution.py:33
  201.3 11.9 %collective-permute-done.37.refs_5_ = bf16[64,4608]{1,0:T(8,128)(2,1)} collective-permute-done((bf16[64,4608]{1,0:T(8,128)(2,1)S(1)}, bf16[64,4608]{1,0:T(8,128)(2,1)}, u32[]{:S(2)}, u32[]{:S(2)}) %collective-permute-start.37) | collective-permute-done | bytes 589856 | tf_op jit(solution)/shard_map/ppermute | solution.py:33
  215.1 9.5 %fusion.refs_12_.refs_8_ = bf16[576,4608]{1,0:T(8,128)(2,1)} fusion(s32[576,9216]{1,0:T(8,128)} %param.5, s32[]{:T(128)S(6)} %select_n.14, bf16[576,9216]{1,0:T(8,128)(2,1)} %param.4), kind=kLoop, calls=%fused_computation.2 | loop fusion | flops 13271040 | bytes 21233668 | tf_op jit(solution)/shard_map/mul | solution.py:279
  230.2 11.9 %collective-permute-done.22.refs_10_ = bf16[64,4608]{1,0:T(8,128)(2,1)} collective-permute-done((bf16[64,4608]{1,0:T(8,128)(2,1)}, bf16[64,4608]{1,0:T(8,128)(2,1)}, u32[]{:S(2)}, u32[]{:S(2)}) %collective-permute-start.22) | collective-permute-done | bytes 589856 | tf_op jit(solution)/shard_map/ppermute | solution.py:17
  243.6 13.7 %product.2 = (f32[2,2,160,576]{3,2,1,0:T(8,128)}, bf16[2,2,160,576]{3,2,1,0:T(8,128)(2,1)}) custom-call(bf16[64,4608]{1,0:T(8,128)(2,1)} %get-tuple-element.46.refs_0_, bf16[64,4608]{1,0:T(8,128)(2,1)} %get-tuple-element.47.refs_1_, bf16[32,4608]{1,0:T(8,128)(2,1)} %get-tuple-element.48.refs_2_, bf16[64,4608]{1,0:T(8,128)(2,1)} %collective-permute-done.15.refs_3_, ...), custom_call_target="tpu_custom_call" | custom-call | flops 6794772480 | bytes 16515072 | tf_op jit(solution)/shard_map/product/pallas_call | solution.py:120
  258.1 9.4 %collective-permute-done.45.refs_4_ = bf16[64,4608]{1,0:T(8,128)(2,1)S(1)} collective-permute-done((bf16[64,4608]{1,0:T(8,128)(2,1)}, bf16[64,4608]{1,0:T(8,128)(2,1)S(1)}, u32[]{:S(2)}, u32[]{:S(2)}) %collective-permute-start.45) | collective-permute-done | bytes 589856 | tf_op jit(solution)/shard_map/ppermute | solution.py:17
  267.6 12.5 %collective-permute-done.47.refs_6_ = bf16[64,4608]{1,0:T(8,128)(2,1)} collective-permute-done((bf16[64,4608]{1,0:T(8,128)(2,1)}, bf16[64,4608]{1,0:T(8,128)(2,1)}, u32[]{:S(2)}, u32[]{:S(2)}) %collective-permute-start.47) | collective-permute-done | bytes 589856 | tf_op jit(solution)/shard_map/ppermute | solution.py:17
  280.1 10.0 %product.3 = (f32[2,2,96,576]{3,2,1,0:T(8,128)}, bf16[2,2,96,576]{3,2,1,0:T(8,128)(2,1)}) custom-call(bf16[64,4608]{1,0:T(8,128)(2,1)} %get-tuple-element.66.refs_0_, bf16[32,4608]{1,0:T(8,128)(2,1)} %get-tuple-element.67.refs_1_, bf16[64,4608]{1,0:T(8,128)(2,1)} %copy-done.57, bf16[32,4608]{1,0:T(8,128)(2,1)} %collective-permute-done.44.refs_3_, ...), custom_call_target="tpu_custom_call" | custom-call | flops 4076863488 | bytes 14155776 | tf_op jit(solution)/shard_map/product/pallas_call | solution.py:120
  358.1 5.2 %collective-permute-done.57 = bf16[4,32,576]{2,1,0:T(8,128)(2,1)S(1)} collective-permute-done((bf16[4,32,576]{2,1,0:T(8,128)(2,1)}, bf16[4,32,576]{2,1,0:T(8,128)(2,1)S(1)}, u32[]{:S(2)}, u32[]{:S(2)}) %collective-permute-start.57) | collective-permute-done | bytes 147488 | tf_op jit(solution)/shard_map/ppermute | solution.py:17
  384.7 7.0 %hessian.1 = f32[576,1152]{1,0:T(8,128)} custom-call(s32[1]{0:T(128)} %bitcast.1.sub_ref, bf16[160,576]{1,0:T(8,128)(2,1)} %total.2.refs_0_, bf16[160,576]{1,0:T(8,128)(2,1)} %copy-done.32, bf16[160,576]{1,0:T(8,128)(2,1)} %copy-done.33, bf16[160,576]{1,0:T(8,128)(2,1)} %copy-done.37, bf16[96,576]{1,0:T(8,128)(2,1)} %total.3.refs_5_.refs_0_.refs_4_, ...), custom_call_target="tpu_custom_call" | custom-call | flops 1358954496 | bytes 2654208 | tf_op jit(solution)/shard_map/hessian/pallas_call | solution.py:193
  (281 shorter events, 154.9 us)
Async XLA Ops:
  12.8 230.1 %collective-permute-start.24 = (bf16[576,4608]{1,0:T(8,128)(2,1)}, bf16[576,4608]{1,0:T(8,128)(2,1)}, u32[]{:S(2)}, u32[]{:S(2)}) collective-permute-start(bf16[576,4608]{1,0:T(8,128)(2,1)} %fusion.1), channel_id=1, source_target_pairs={{0,1},{1,0},{2,3},{3,2},{4,5},{5,4},{6,7},{7,6},{8,9},{9,8},{10,11... | collective-permute-start | bytes 15925256 | tf_op jit(solution)/shard_map/ppermute | solution.py:17
  23.6 30.0 %collective-permute-start.11 = (bf16[32,4608]{1,0:T(8,128)(2,1)}, bf16[32,4608]{1,0:T(8,128)(2,1)}, u32[]{:S(2)}, u32[]{:S(2)}) collective-permute-start(bf16[32,4608]{1,0:T(8,128)(2,1)} %get-tuple-element.91.refs_0_), channel_id=1, source_target_pairs={{0,4},{6,2},{1,5},{7,3},{8,12},{14,10},{9,13},{15,11},{16,20},{22,... | collective-permute-start | bytes 884744 | tf_op jit(solution)/shard_map/ppermute | solution.py:25
  31.1 42.5 %collective-permute-start.35 = (bf16[64,4608]{1,0:T(8,128)(2,1)S(1)}, bf16[64,4608]{1,0:T(8,128)(2,1)S(1)}, u32[]{:S(2)}, u32[]{:S(2)}) collective-permute-start(bf16[64,4608]{1,0:T(8,128)(2,1)S(1)} %get-tuple-element.92.refs_0_), channel_id=1, source_target_pairs={{2,4},{4,2},{3,5},{5,3},{10,12},{12,10},{11,13},{13,11},{18,20},{2... | collective-permute-start | bytes 1769480 | tf_op jit(solution)/shard_map/ppermute | solution.py:24
  36.0 40.3 %collective-permute-start.34 = (bf16[64,4608]{1,0:T(8,128)(2,1)S(1)}, bf16[64,4608]{1,0:T(8,128)(2,1)S(1)}, u32[]{:S(2)}, u32[]{:S(2)}) collective-permute-start(bf16[64,4608]{1,0:T(8,128)(2,1)S(1)} %get-tuple-element.92.refs_0_), channel_id=1, source_target_pairs={{0,4},{6,2},{1,5},{7,3},{8,12},{14,10},{9,13},{15,11},{16,20},{22,... | collective-permute-start | bytes 1769480 | tf_op jit(solution)/shard_map/ppermute | solution.py:25
  41.4 35.6 %collective-permute-start.33 = (bf16[64,4608]{1,0:T(8,128)(2,1)S(1)}, bf16[64,4608]{1,0:T(8,128)(2,1)S(1)}, u32[]{:S(2)}, u32[]{:S(2)}) collective-permute-start(bf16[64,4608]{1,0:T(8,128)(2,1)S(1)} %get-tuple-element.92.refs_0_), channel_id=1, source_target_pairs={{0,2},{2,0},{4,6},{6,4},{1,3},{3,1},{5,7},{7,5},{8,10},{10,8},{12,... | collective-permute-start | bytes 1769480 | tf_op jit(solution)/shard_map/ppermute | solution.py:26
  73.6 28.5 %collective-permute-start = (bf16[64,4608]{1,0:T(8,128)(2,1)S(1)}, bf16[64,4608]{1,0:T(8,128)(2,1)}, u32[]{:S(2)}, u32[]{:S(2)}) collective-permute-start(bf16[64,4608]{1,0:T(8,128)(2,1)S(1)} %get-tuple-element.94.refs_0_), channel_id=1, source_target_pairs={{0,2},{2,0},{4,6},{6,4},{1,3},{3,1},{5,7},{7,5},{8,10},{10,8},{12,... | collective-permute-start | bytes 1769480 | tf_op jit(solution)/shard_map/ppermute | solution.py:26
  76.3 26.5 %collective-permute-start.2 = (bf16[64,4608]{1,0:T(8,128)(2,1)S(1)}, bf16[64,4608]{1,0:T(8,128)(2,1)S(1)}, u32[]{:S(2)}, u32[]{:S(2)}) collective-permute-start(bf16[64,4608]{1,0:T(8,128)(2,1)S(1)} %get-tuple-element.94.refs_0_), channel_id=1, source_target_pairs={{2,4},{4,2},{3,5},{5,3},{10,12},{12,10},{11,13},{13,11},{18,20},{2... | collective-permute-start | bytes 1769480 | tf_op jit(solution)/shard_map/ppermute | solution.py:24
  77.0 33.8 %collective-permute-start.1 = (bf16[64,4608]{1,0:T(8,128)(2,1)S(1)}, bf16[64,4608]{1,0:T(8,128)(2,1)S(1)}, u32[]{:S(2)}, u32[]{:S(2)}) collective-permute-start(bf16[64,4608]{1,0:T(8,128)(2,1)S(1)} %get-tuple-element.94.refs_0_), channel_id=1, source_target_pairs={{0,4},{6,2},{1,5},{7,3},{8,12},{14,10},{9,13},{15,11},{16,20},{22,... | collective-permute-start | bytes 1769480 | tf_op jit(solution)/shard_map/ppermute | solution.py:25
  102.1 30.0 %collective-permute-start.7 = (bf16[64,4608]{1,0:T(8,128)(2,1)S(1)}, bf16[64,4608]{1,0:T(8,128)(2,1)S(1)}, u32[]{:S(2)}, u32[]{:S(2)}) collective-permute-start(bf16[64,4608]{1,0:T(8,128)(2,1)S(1)} %get-tuple-element.93.refs_0_), channel_id=1, source_target_pairs={{2,4},{4,2},{3,5},{5,3},{10,12},{12,10},{11,13},{13,11},{18,20},{2... | collective-permute-start | bytes 1769480 | tf_op jit(solution)/shard_map/ppermute | solution.py:24
  102.8 30.6 %collective-permute-start.6 = (bf16[64,4608]{1,0:T(8,128)(2,1)S(1)}, bf16[64,4608]{1,0:T(8,128)(2,1)}, u32[]{:S(2)}, u32[]{:S(2)}) collective-permute-start(bf16[64,4608]{1,0:T(8,128)(2,1)S(1)} %get-tuple-element.93.refs_0_), channel_id=1, source_target_pairs={{0,4},{6,2},{1,5},{7,3},{8,12},{14,10},{9,13},{15,11},{16,20},{22,... | collective-permute-start | bytes 1769480 | tf_op jit(solution)/shard_map/ppermute | solution.py:25
  135.4 27.6 %collective-permute-start.4 = (bf16[64,4608]{1,0:T(8,128)(2,1)}, bf16[64,4608]{1,0:T(8,128)(2,1)S(1)}, u32[]{:S(2)}, u32[]{:S(2)}) collective-permute-start(bf16[64,4608]{1,0:T(8,128)(2,1)} %copy-done.14), channel_id=1, source_target_pairs={{2,0},{4,6},{3,1},{5,7},{10,8},{12,14},{11,9},{13,15},{18,16},{20,... | collective-permute-start | bytes 1769480 | tf_op jit(solution)/shard_map/ppermute | solution.py:33
  136.8 39.0 %collective-permute-start.8 = (bf16[64,4608]{1,0:T(8,128)(2,1)S(1)}, bf16[64,4608]{1,0:T(8,128)(2,1)}, u32[]{:S(2)}, u32[]{:S(2)}) collective-permute-start(bf16[64,4608]{1,0:T(8,128)(2,1)S(1)} %collective-permute-done.7.refs_3_), channel_id=1, source_target_pairs={{2,0},{4,6},{3,1},{5,7},{10,8},{12,14},{11,9},{13,15},{18,16},{20,... | collective-permute-start | bytes 1769480 | tf_op jit(solution)/shard_map/ppermute | solution.py:33
  143.2 45.2 %collective-permute-start.9 = (bf16[64,4608]{1,0:T(8,128)(2,1)}, bf16[64,4608]{1,0:T(8,128)(2,1)}, u32[]{:S(2)}, u32[]{:S(2)}) collective-permute-start(bf16[64,4608]{1,0:T(8,128)(2,1)} %collective-permute-done.6.refs_2_), channel_id=1, source_target_pairs={{2,0},{4,6},{3,1},{5,7},{10,8},{12,14},{11,9},{13,15},{18,16},{20,... | collective-permute-start | bytes 1769480 | tf_op jit(solution)/shard_map/ppermute | solution.py:33
  163.8 37.2 %collective-permute-start.36 = (bf16[64,4608]{1,0:T(8,128)(2,1)S(1)}, bf16[64,4608]{1,0:T(8,128)(2,1)}, u32[]{:S(2)}, u32[]{:S(2)}) collective-permute-start(bf16[64,4608]{1,0:T(8,128)(2,1)S(1)} %collective-permute-done.35.refs_3_), channel_id=1, source_target_pairs={{2,0},{4,6},{3,1},{5,7},{10,8},{12,14},{11,9},{13,15},{18,16},{20,... | collective-permute-start | bytes 1769480 | tf_op jit(solution)/shard_map/ppermute | solution.py:33
  168.4 44.8 %collective-permute-start.37 = (bf16[64,4608]{1,0:T(8,128)(2,1)S(1)}, bf16[64,4608]{1,0:T(8,128)(2,1)}, u32[]{:S(2)}, u32[]{:S(2)}) collective-permute-start(bf16[64,4608]{1,0:T(8,128)(2,1)S(1)} %collective-permute-done.34.refs_2_), channel_id=1, source_target_pairs={{2,0},{4,6},{3,1},{5,7},{10,8},{12,14},{11,9},{13,15},{18,16},{20,... | collective-permute-start | bytes 1769480 | tf_op jit(solution)/shard_map/ppermute | solution.py:33
  175.8 37.5 %collective-permute-start.15 = (bf16[64,4608]{1,0:T(8,128)(2,1)}, bf16[64,4608]{1,0:T(8,128)(2,1)}, u32[]{:S(2)}, u32[]{:S(2)}) collective-permute-start(bf16[64,4608]{1,0:T(8,128)(2,1)} %get-tuple-element.49), channel_id=1, source_target_pairs={{0,8},{8,0},{16,24},{24,16},{1,9},{9,1},{17,25},{25,17},{2,10},{10... | collective-permute-start | bytes 1769480 | tf_op jit(solution)/shard_map/ppermute | solution.py:17
  188.4 26.3 %collective-permute-start.18 = (bf16[64,4608]{1,0:T(8,128)(2,1)}, bf16[64,4608]{1,0:T(8,128)(2,1)}, u32[]{:S(2)}, u32[]{:S(2)}) collective-permute-start(bf16[64,4608]{1,0:T(8,128)(2,1)} %get-tuple-element.52), channel_id=1, source_target_pairs={{0,16},{8,24},{16,0},{24,8},{1,17},{9,25},{17,1},{25,9},{2,18},{10... | collective-permute-start | bytes 1769480 | tf_op jit(solution)/shard_map/ppermute | solution.py:17
  201.0 26.9 %collective-permute-start.21 = (bf16[64,4608]{1,0:T(8,128)(2,1)}, bf16[64,4608]{1,0:T(8,128)(2,1)S(1)}, u32[]{:S(2)}, u32[]{:S(2)}) collective-permute-start(bf16[64,4608]{1,0:T(8,128)(2,1)} %get-tuple-element.55), channel_id=1, source_target_pairs={{0,24},{8,16},{16,8},{24,0},{1,25},{9,17},{17,9},{25,1},{2,26},{10... | collective-permute-start | bytes 1769480 | tf_op jit(solution)/shard_map/ppermute | solution.py:17
  214.7 27.4 %collective-permute-start.22 = (bf16[64,4608]{1,0:T(8,128)(2,1)}, bf16[64,4608]{1,0:T(8,128)(2,1)}, u32[]{:S(2)}, u32[]{:S(2)}) collective-permute-start(bf16[64,4608]{1,0:T(8,128)(2,1)} %get-tuple-element.56), channel_id=1, source_target_pairs={{0,24},{8,16},{16,8},{24,0},{1,25},{9,17},{17,9},{25,1},{2,26},{10... | collective-permute-start | bytes 1769480 | tf_op jit(solution)/shard_map/ppermute | solution.py:17
  228.0 29.4 %collective-permute-start.46 = (bf16[32,4608]{1,0:T(8,128)(2,1)}, bf16[32,4608]{1,0:T(8,128)(2,1)S(1)}, u32[]{:S(2)}, u32[]{:S(2)}) collective-permute-start(bf16[32,4608]{1,0:T(8,128)(2,1)} %get-tuple-element.71), channel_id=1, source_target_pairs={{0,16},{8,24},{16,0},{24,8},{1,17},{9,25},{17,1},{25,9},{2,18},{10... | collective-permute-start | bytes 884744 | tf_op jit(solution)/shard_map/ppermute | solution.py:17
  229.5 28.6 %collective-permute-start.48 = (bf16[32,4608]{1,0:T(8,128)(2,1)}, bf16[32,4608]{1,0:T(8,128)(2,1)}, u32[]{:S(2)}, u32[]{:S(2)}) collective-permute-start(bf16[32,4608]{1,0:T(8,128)(2,1)} %get-tuple-element.73), channel_id=1, source_target_pairs={{0,24},{8,16},{16,8},{24,0},{1,25},{9,17},{17,9},{25,1},{2,26},{10... | collective-permute-start | bytes 884744 | tf_op jit(solution)/shard_map/ppermute | solution.py:17
  229.7 28.4 %collective-permute-start.43 = (bf16[64,4608]{1,0:T(8,128)(2,1)}, bf16[64,4608]{1,0:T(8,128)(2,1)S(1)}, u32[]{:S(2)}, u32[]{:S(2)}) collective-permute-start(bf16[64,4608]{1,0:T(8,128)(2,1)} %get-tuple-element.68), channel_id=1, source_target_pairs={{0,8},{8,0},{16,24},{24,16},{1,9},{9,1},{17,25},{25,17},{2,10},{10... | collective-permute-start | bytes 1769480 | tf_op jit(solution)/shard_map/ppermute | solution.py:17
  242.9 37.1 %collective-permute-start.47 = (bf16[64,4608]{1,0:T(8,128)(2,1)}, bf16[64,4608]{1,0:T(8,128)(2,1)}, u32[]{:S(2)}, u32[]{:S(2)}) collective-permute-start(bf16[64,4608]{1,0:T(8,128)(2,1)} %get-tuple-element.72), channel_id=1, source_target_pairs={{0,24},{8,16},{16,8},{24,0},{1,25},{9,17},{17,9},{25,1},{2,26},{10... | collective-permute-start | bytes 1769480 | tf_op jit(solution)/shard_map/ppermute | solution.py:17
  257.3 41.3 %collective-permute-start.25 = (bf16[2,2,160,576]{3,2,1,0:T(8,128)(2,1)}, bf16[2,2,160,576]{3,2,1,0:T(8,128)(2,1)S(1)}, u32[]{:S(2)}, u32[]{:S(2)}) collective-permute-start(bf16[2,2,160,576]{3,2,1,0:T(8,128)(2,1)} %get-tuple-element.61), channel_id=1, source_target_pairs={{0,8},{8,0},{16,24},{24,16},{1,9},{9,1},{17,25},{25,17},{2,10},{10... | collective-permute-start | bytes 2211848 | tf_op jit(solution)/shard_map/ppermute | solution.py:17
  (116 other events, 2600.0 us)
